TPU v7x, 32 devices: a whole 2x2x4 slice. The times are simulated.
32 devices in a mesh: dp: 4 (over x, y), sp: 8 (over z, core).
Axes of the slice: x: 2, y: 2, z: 4, core: 2. Of those that a mesh axis runs over, the one named last changes fastest.
Arguments:
- hidden_in: bfloat16 [8192, 3072], P(('dp', 'sp')), parts along dimension 0
- positions: int32 [8192], P(('dp', 'sp')), parts along dimension 0
- g_kv: bfloat16 [3072], replicated
- w_k: bfloat16 [3072, 3072], replicated
- w_v: bfloat16 [3072, 3072], replicated
- g_attn: bfloat16 [2, 3072], replicated
- w_q: bfloat16 [2, 3072, 3072], replicated
- w_o: bfloat16 [2, 32, 96, 3072], replicated
- g_mlp: bfloat16 [2, 3072], replicated
- w_gate: bfloat16 [2, 3072, 8192], replicated
- w_up: bfloat16 [2, 3072, 8192], replicated
- w_down: bfloat16 [2, 8192, 3072], replicated
Outputs:
- output: bfloat16 [8192, 3072], P(('dp', 'sp')), parts along dimension 0
There are 4 independent parts. A program takes and returns all parts, laid end to end along the dimension named above; an argument that names none is the same for every part.
All inputs are finite; a program needn't handle non-finite values.
Results may differ from a plain program's by a relative error of at most 0.02.
Values are sent between devices in bfloat16 or wider.
A program may use at most 1.75 GiB of HBM per device.

v0:
```python
import jax
import jax.numpy as jnp
from jax import lax
from jax.sharding import PartitionSpec as P

NORM_EPS = 1e-6


def rms_norm(rows, gain):
    rows32 = rows.astype(jnp.float32)
    inv_rms = lax.rsqrt(jnp.mean(rows32 * rows32, axis=-1, keepdims=True) + NORM_EPS)
    return (rows32 * inv_rms * gain.astype(jnp.float32)).astype(jnp.bfloat16)


def decoder_layers(hidden, allowed, all_k, all_v, g_attn, w_q, w_o, g_mlp, w_gate, w_up, w_down):
    tokens, width = hidden.shape
    layers, heads, head_dim, _ = w_o.shape
    kv_heads = all_k.shape[1]
    group = heads // kv_heads
    scale = head_dim ** -0.5
    for layer in range(layers):
        queries = jnp.dot(rms_norm(hidden, g_attn[layer]), w_q[layer], preferred_element_type=jnp.float32).astype(jnp.bfloat16).reshape(tokens, group, kv_heads, head_dim)
        scores = jnp.einsum('qrgd,kgd->rgqk', queries, all_k, preferred_element_type=jnp.float32) * scale
        scores = jnp.where(allowed, scores, -jnp.inf)
        attn_probs = jax.nn.softmax(scores, axis=-1).astype(jnp.bfloat16)
        attn_out = jnp.einsum('rgqk,kgd->qrgd', attn_probs, all_v, preferred_element_type=jnp.float32).astype(jnp.bfloat16).reshape(tokens, heads * head_dim)
        attn_proj = jnp.dot(attn_out, w_o[layer].reshape(heads * head_dim, width), preferred_element_type=jnp.float32).astype(jnp.bfloat16)
        hidden = (hidden.astype(jnp.float32) + attn_proj.astype(jnp.float32)).astype(jnp.bfloat16)
        normed_m = rms_norm(hidden, g_mlp[layer])
        gate = jnp.dot(normed_m, w_gate[layer], preferred_element_type=jnp.float32).astype(jnp.bfloat16)
        upper = jnp.dot(normed_m, w_up[layer], preferred_element_type=jnp.float32).astype(jnp.bfloat16)
        mlp_act = (jax.nn.silu(gate.astype(jnp.float32)) * upper.astype(jnp.float32)).astype(jnp.bfloat16)
        down_proj = jnp.dot(mlp_act, w_down[layer], preferred_element_type=jnp.float32).astype(jnp.bfloat16)
        hidden = (hidden.astype(jnp.float32) + down_proj.astype(jnp.float32)).astype(jnp.bfloat16)
    return hidden


def solution(mesh):
    row_spec = P(('dp', 'sp'), None)
    pos_spec = P(('dp', 'sp'))
    full = P()

    def local_step(rows_in, pos_rows, g_kv, w_k, w_v, g_attn, w_q, w_o, g_mlp, w_gate, w_up, w_down):
        head_dim = w_o.shape[2]
        kv_heads = w_k.shape[1] // head_dim
        normed = rms_norm(rows_in, g_kv)
        local_k = jnp.dot(normed, w_k, preferred_element_type=jnp.float32).astype(jnp.bfloat16)
        local_v = jnp.dot(normed, w_v, preferred_element_type=jnp.float32).astype(jnp.bfloat16)
        all_k = lax.all_gather(local_k, 'sp', axis=0, tiled=True)
        all_v = lax.all_gather(local_v, 'sp', axis=0, tiled=True)
        all_pos = lax.all_gather(pos_rows, 'sp', axis=0, tiled=True)
        seq_len = all_k.shape[0]
        all_k = all_k.reshape(seq_len, kv_heads, head_dim)
        all_v = all_v.reshape(seq_len, kv_heads, head_dim)
        allowed = all_pos[None, :] <= pos_rows[:, None]
        return decoder_layers(rows_in, allowed, all_k, all_v, g_attn, w_q, w_o, g_mlp, w_gate, w_up, w_down)

    return jax.shard_map(local_step, mesh=mesh, in_specs=(row_spec, pos_spec, full, full, full, full, full, full, full, full, full, full), out_specs=row_spec, check_vma=False)
```

profile of v0, /device:TPU:0, one launch (start us, length us, event | category | flops | bytes accessed | tf_op | source)
XLA Modules:
  0.0 562.5 jit_solution(10710092303544810278)
XLA Ops:
  6.5 1.8 fusion.156
  8.3 0.7 convert_element_type.146
  9.0 13.0 %convolution_convert_fusion = bf16[256,3072]{1,0:T(8,128)(2,1)} fusion(bf16[3072,3072]{1,0:T(8,128)(2,1)} %param.15, bf16[256,3072]{1,0:T(8,128)(2,1)} %param.12, f32[3072]{0:T(1024)S(1)} %convert_element_type.146, f32[256]{0:T(256)S(1)} %add_rsqrt_fusion.3), kind=kOutput, calls=%fused_computation.88 | convolution fusion | flops 4835770368 | bytes 22033408 | tf_op jit(solution)/shard_map/dot_general | solution.py:47
  22.1 0.0 all-gather.4.cloned.1.call-start
  22.1 10.5 %convolution_convert_fusion.1 = bf16[256,3072]{1,0:T(8,128)(2,1)} fusion(bf16[3072,3072]{1,0:T(8,128)(2,1)} %param.16, bf16[256,3072]{1,0:T(8,128)(2,1)S(1)} %copy-done, f32[3072]{0:T(1024)S(1)} %convert_element_type.146, f32[256]{0:T(256)S(1)} %add_rsqrt_fusion.3), kind=kOutput, calls=%fused_computation.89 | convolution fusion | flops 4835770368 | bytes 22033408 | tf_op jit(solution)/shard_map/dot_general | solution.py:48
  32.7 0.6 slice_convert_fusion.1
  33.3 10.0 %fusion.108 = bf16[256,3072]{1,0:T(8,128)(2,1)} fusion(bf16[2,3072,3072]{2,1,0:T(8,128)(2,1)} %param.18, bf16[256,3072]{1,0:T(8,128)(2,1)S(1)} %copy-done, f32[3072]{0:T(1024)S(1)} %bitcast.242, f32[256]{0:T(256)S(1)} %add_rsqrt_fusion.3), kind=kOutput, calls=%fused_computation.86 | convolution fusion | flops 4835770368 | bytes 22033408 | tf_op jit(solution)/shard_map/dot_general | solution.py:22
  43.3 1.7 copy.29
  45.0 14.1 %all-gather = s32[8,1,256]{2,1,0:T(1,128)S(1)} all-gather(s32[1,1,256]{2,1,0:T(1,128)S(1)} %bitcast.243), channel_id=1, replica_groups=mesh['dp'=4,'sp'=8] {'sp'}, dimensions={0}, use_global_device_ids=true | all-gather | bytes 9216 | tf_op jit(solution)/shard_map/all_gather | solution.py:51
  59.1 0.4 broadcast_compare_fusion
  59.5 0.6 slice_convert_fusion
  60.2 81.2 %all-gather.6.cloned.1.call-done = bf16[2048,3072]{1,0:T(8,128)(2,1)} async-done(((bf16[256,3072]{1,0:T(8,128)(2,1)}), bf16[2048,3072]{1,0:T(8,128)(2,1)}) %all-gather.6.cloned.1.call-update) | async-done | bytes 12582928 | tf_op jit(solution)/shard_map/all_gather | solution.py:49
  141.4 16.7 %copy.28 = bf16[2048,3072]{0,1:T(8,128)(2,1)} copy(bf16[2048,3072]{1,0:T(8,128)(2,1)} %all-gather.6.cloned.1.call-done) | data formatting | bytes 25165824 | tf_op jit(solution)/shard_map/all_gather | solution.py:49
  158.0 28.2 %fusion.2 = (f32[32,256]{1,0:T(8,128)S(1)}, f32[32,2048,256]{2,1,0:T(8,128)}) fusion(pred[256,2048]{0,1:T(8,128)(4,1)S(1)} %broadcast_compare_fusion, bf16[2048,32,96]{0,2,1:T(8,128)(2,1)} %bitcast.230, bf16[256,32,96]{0,2,1:T(8,128)(2,1)S(1)} %bitcast.234), kind=kOutput, calls=%fused_computation.8 | convolution fusion | flops 3271548928 | bytes 81821696 | tf_op jit(solution)/shard_map/qrgd,kgd->rgqk/dot_general | solution.py:23
  186.2 21.6 %fusion = f32[32,256]{1,0:T(8,128)S(1)} fusion(f32[32,2048,256]{2,1,0:T(8,128)} %get-tuple-element.10, f32[32,256]{1,0:T(8,128)S(1)} %get-tuple-element.9, pred[256,2048]{0,1:T(8,128)(4,1)S(1)} %broadcast_compare_fusion), kind=kLoop, calls=%fused_computation.6 | loop fusion | flops 67100672 | bytes 67698688 | tf_op jit(solution)/shard_map/reduce_sum | solution.py:25
  207.8 50.2 %all-gather.4.cloned.1.call-done = bf16[2048,3072]{1,0:T(8,128)(2,1)} async-done(((bf16[256,3072]{1,0:T(8,128)(2,1)}), bf16[2048,3072]{1,0:T(8,128)(2,1)}) %all-gather.4.cloned.1.call-update) | async-done | bytes 12582928 | tf_op jit(solution)/shard_map/all_gather | solution.py:50
  258.0 16.7 %copy.27 = bf16[2048,3072]{0,1:T(8,128)(2,1)} copy(bf16[2048,3072]{1,0:T(8,128)(2,1)} %all-gather.4.cloned.1.call-done) | data formatting | bytes 25165824 | tf_op jit(solution)/shard_map/all_gather | solution.py:50
  274.7 29.9 %fusion.172 = bf16[32,96,256]{2,1,0:T(8,128)(2,1)} fusion(bf16[2048,32,96]{0,2,1:T(8,128)(2,1)} %bitcast.232, f32[32,256]{1,0:T(8,128)S(1)} %fusion, f32[32,256]{1,0:T(8,128)S(1)} %get-tuple-element.9, f32[32,2048,256]{2,1,0:T(8,128)} %get-tuple-element.10, pred[256,2048]{0,1:T(8,128)(4,1)S(1)} %broadcast_compare_fusion), kind=kOutput, calls=%fused_computation.110 | convolution fusion | flops 3305897984 | bytes 81854464 | tf_op jit(solution)/shard_map/rgqk,kgd->qrgd/dot_general | solution.py:26
  304.6 10.5 %fusion.157 = (f32[256]{0:T(256)S(1)}, bf16[256,3072]{1,0:T(8,128)(2,1)}) fusion(bf16[2,32,96,3072]{3,2,1,0:T(8,128)(2,1)} %param.19, bf16[32,96,256]{2,1,0:T(8,128)(2,1)} %fusion.172, bf16[256,3072]{1,0:T(8,128)(2,1)S(1)} %copy-done.1), kind=kOutput, calls=%fused_computation.101 | convolution fusion | flops 4838129664 | bytes 23593984 | tf_op jit(solution)/shard_map/dot_general | solution.py:27
  315.1 23.1 %fusion.38 = bf16[256,8192]{1,0:T(8,128)(2,1)} fusion(bf16[2,3072,8192]{2,1,0:T(8,128)(2,1)} %param.21, bf16[256,3072]{1,0:T(8,128)(2,1)} %get-tuple-element.12, f32[3072]{0:T(1024)S(1)} %bitcast.240, f32[256]{0:T(256)S(1)} %add_rsqrt_fusion.2), kind=kOutput, calls=%fused_computation.48 | convolution fusion | flops 12890144768 | bytes 56112128 | tf_op jit(solution)/shard_map/dot_general | solution.py:30
  338.2 23.2 %fusion.65.clone.9.clone.5 = bf16[256,8192]{1,0:T(8,128)(2,1)} fusion(bf16[2,3072,8192]{2,1,0:T(8,128)(2,1)} %param.22, bf16[256,8192]{1,0:T(8,128)(2,1)} %fusion.38, bf16[256,3072]{1,0:T(8,128)(2,1)} %get-tuple-element.12, f32[3072]{0:T(1024)S(1)} %bitcast.241, f32[256]{0:T(256)S(1)} %add_rsqrt_fusion.2), kind=kOutput, calls=%fused_computation.57.clone.clone.clone.clone.clone.clone.clone.clone.clone.clone... | convolution fusion | flops 12906921984 | bytes 60306432 | tf_op jit(solution)/shard_map/dot_general | solution.py:31
  361.5 22.3 %fusion.160 = (f32[256]{0:T(256)S(1)}, bf16[256,3072]{1,0:T(8,128)(2,1)S(1)}) fusion(bf16[2,8192,3072]{2,1,0:T(8,128)(2,1)} %param.23, bf16[256,3072]{1,0:T(8,128)(2,1)} %get-tuple-element.12, bf16[256,8192]{1,0:T(8,128)(2,1)} %fusion.65.clone.9.clone.5), kind=kOutput, calls=%fused_computation.104 | convolution fusion | flops 12891193344 | bytes 57672704 | tf_op jit(solution)/shard_map/dot_general | solution.py:33
  383.8 1.2 copy-done.8
  385.0 9.9 %fusion.111 = bf16[256,3072]{1,0:T(8,128)(2,1)} fusion(bf16[2,3072,3072]{2,1,0:T(8,128)(2,1)} %param.18, bf16[256,3072]{1,0:T(8,128)(2,1)S(1)} %get-tuple-element.14, f32[3072]{0:T(1024)S(1)} %bitcast.239, f32[256]{0:T(256)S(1)} %add_rsqrt_fusion.1), kind=kOutput, calls=%fused_computation.87 | convolution fusion | flops 4835770368 | bytes 22033408 | tf_op jit(solution)/shard_map/dot_general | solution.py:22
  394.9 1.7 copy.31
  396.6 28.4 %fusion.3 = (f32[32,256]{1,0:T(8,128)S(1)}, f32[32,2048,256]{2,1,0:T(8,128)}) fusion(pred[256,2048]{0,1:T(8,128)(4,1)S(1)} %broadcast_compare_fusion, bf16[2048,32,96]{0,2,1:T(8,128)(2,1)} %bitcast.231, bf16[256,32,96]{0,2,1:T(8,128)(2,1)S(1)} %bitcast.235), kind=kOutput, calls=%fused_computation.9 | convolution fusion | flops 3271548928 | bytes 81821696 | tf_op jit(solution)/shard_map/qrgd,kgd->rgqk/dot_general | solution.py:23
  425.0 21.6 %fusion.1 = f32[32,256]{1,0:T(8,128)S(1)} fusion(f32[32,2048,256]{2,1,0:T(8,128)} %get-tuple-element.16, f32[32,256]{1,0:T(8,128)S(1)} %get-tuple-element.15, pred[256,2048]{0,1:T(8,128)(4,1)S(1)} %broadcast_compare_fusion), kind=kLoop, calls=%fused_computation.7 | loop fusion | flops 67100672 | bytes 67698688 | tf_op jit(solution)/shard_map/reduce_sum | solution.py:25
  446.6 29.8 %fusion.175 = bf16[32,96,256]{2,1,0:T(8,128)(2,1)} fusion(bf16[2048,32,96]{0,2,1:T(8,128)(2,1)} %bitcast.233, f32[32,256]{1,0:T(8,128)S(1)} %fusion.1, f32[32,256]{1,0:T(8,128)S(1)} %get-tuple-element.15, f32[32,2048,256]{2,1,0:T(8,128)} %get-tuple-element.16, pred[256,2048]{0,1:T(8,128)(4,1)S(1)} %broadcast_compare_fusion), kind=kOutput, calls=%fused_computation.111 | convolution fusion | flops 3305897984 | bytes 81854464 | tf_op jit(solution)/shard_map/rgqk,kgd->qrgd/dot_general | solution.py:26
  476.4 10.1 %fusion.163 = (f32[256]{0:T(256)S(1)}, bf16[256,3072]{1,0:T(8,128)(2,1)S(1)}) fusion(bf16[2,32,96,3072]{3,2,1,0:T(8,128)(2,1)} %param.19, bf16[32,96,256]{2,1,0:T(8,128)(2,1)} %fusion.175, bf16[256,3072]{1,0:T(8,128)(2,1)} %copy-done.8), kind=kOutput, calls=%fused_computation.107 | convolution fusion | flops 4838129664 | bytes 23593984 | tf_op jit(solution)/shard_map/dot_general | solution.py:27
  486.5 22.9 %fusion.50 = bf16[256,8192]{1,0:T(8,128)(2,1)} fusion(bf16[2,3072,8192]{2,1,0:T(8,128)(2,1)} %param.21, bf16[256,3072]{1,0:T(8,128)(2,1)S(1)} %get-tuple-element.18, f32[3072]{0:T(1024)S(1)} %bitcast.237, f32[256]{0:T(256)S(1)} %add_rsqrt_fusion), kind=kOutput, calls=%fused_computation.52 | convolution fusion | flops 12890144768 | bytes 56112128 | tf_op jit(solution)/shard_map/dot_general | solution.py:30
  509.4 22.8 %fusion.62.clone.13 = bf16[256,8192]{1,0:T(8,128)(2,1)} fusion(bf16[2,3072,8192]{2,1,0:T(8,128)(2,1)} %param.22, bf16[256,8192]{1,0:T(8,128)(2,1)} %fusion.50, bf16[256,3072]{1,0:T(8,128)(2,1)S(1)} %get-tuple-element.18, f32[3072]{0:T(1024)S(1)} %bitcast.238, f32[256]{0:T(256)S(1)} %add_rsqrt_fusion), kind=kOutput, calls=%fused_computation.56.clone.clone.clone.clone.clone.clone.clone.clone.clone.clone... | convolution fusion | flops 12906921984 | bytes 60306432 | tf_op jit(solution)/shard_map/dot_general | solution.py:31
  532.2 23.0 %fusion.147 = bf16[256,3072]{1,0:T(8,128)(2,1)} fusion(bf16[2,8192,3072]{2,1,0:T(8,128)(2,1)} %param.23, bf16[256,3072]{1,0:T(8,128)(2,1)S(1)} %get-tuple-element.18, bf16[256,8192]{1,0:T(8,128)(2,1)} %fusion.62.clone.13), kind=kOutput, calls=%fused_computation.95 | convolution fusion | flops 12888834048 | bytes 57671680 | tf_op jit(solution)/shard_map/dot_general | solution.py:33
  (24 shorter events, 0.1 us)
Async XLA Ops:
  6.5 134.8 %all-gather.6.cloned.1.call-start = ((), (), s32[]{:S(2)}) async-start(), calls=%async_computation.1 | async-start | bytes 14155776 | tf_op jit(solution)/shard_map/all_gather | solution.py:49
  9.0 13.1 %copy-start = (bf16[256,3072]{1,0:T(8,128)(2,1)S(1)}, bf16[256,3072]{1,0:T(8,128)(2,1)}, u32[]{:S(2)}) copy-start(bf16[256,3072]{1,0:T(8,128)(2,1)} %param.12) | copy-start | bytes 4718596
  22.1 10.6 %copy-start.2 = (bf16[2,3072]{1,0:T(2,128)(2,1)S(1)}, bf16[2,3072]{1,0:T(2,128)(2,1)}, u32[]{:S(2)}) copy-start(bf16[2,3072]{1,0:T(2,128)(2,1)} %param.17) | copy-start | bytes 36868
  22.1 236.0 %all-gather.4.cloned.1.call-start = ((), (), s32[]{:S(2)}) async-start(), calls=%async_computation | async-start | bytes 14155776 | tf_op jit(solution)/shard_map/all_gather | solution.py:50
  33.3 11.7 %copy-start.7 = (s32[256]{0:T(256)S(1)}, s32[256]{0:T(256)}, u32[]{:S(2)}) copy-start(s32[256]{0:T(256)} %param.13) | copy-start | bytes 3076
  33.3 26.2 %copy-start.3 = (bf16[2,3072]{1,0:T(2,128)(2,1)S(1)}, bf16[2,3072]{1,0:T(2,128)(2,1)}, u32[]{:S(2)}) copy-start(bf16[2,3072]{1,0:T(2,128)(2,1)} %param.20) | copy-start | bytes 36868
  274.7 29.9 %copy-start.1 = (bf16[256,3072]{1,0:T(8,128)(2,1)S(1)}, bf16[256,3072]{1,0:T(8,128)(2,1)}, u32[]{:S(2)}) copy-start(bf16[256,3072]{1,0:T(8,128)(2,1)} %param.12) | copy-start | bytes 4718596
  304.6 10.5 %copy-start.6 = (f32[1,3072]{1,0:T(1,128)S(1)}, f32[1,3072]{1,0:T(1,128)}, u32[]{:S(2)}) copy-start(f32[1,3072]{1,0:T(1,128)} %get-tuple-element.6) | copy-start | bytes 36868
  361.5 23.5 %copy-start.5 = (f32[1,3072]{1,0:T(1,128)S(1)}, f32[1,3072]{1,0:T(1,128)}, u32[]{:S(2)}) copy-start(f32[1,3072]{1,0:T(1,128)} %get-tuple-element.7) | copy-start | bytes 36868
  383.8 1.2 copy-start.8
  476.4 10.1 %copy-start.4 = (f32[1,3072]{1,0:T(1,128)S(1)}, f32[1,3072]{1,0:T(1,128)}, u32[]{:S(2)}) copy-start(f32[1,3072]{1,0:T(1,128)} %get-tuple-element.5) | copy-start | bytes 36868
Sparse Core Ops, SparseCore 0:
  22.2 119.1 all-gather.5
  143.0 115.0 all-gather.3
where the time goes:
time: 569 us; the launch traced here: 562 us
  matrix products  318 us (56%)
  waiting for transfers between devices  131 us (23%)
  other arithmetic  47.4 us (8%)
  local copies, waits for them, and re-layouts  38 us (7%)
  blocking collectives  14.1 us (2%)
  between operations  14 us (2%)
    all_gather x1, waiting for transfers between devices, local_step(): all_k = lax.all_gather(local_k, 'sp', axis=0, tiled=True)  81.2 us
    dot_general x2, matrix products, decoder_layers(): jnp.einsum('rgqk,kgd->qrgd', attn_probs, all_v, preferred_element_type=jn...  59.7 us
    dot_general x2, matrix products, decoder_layers(): jnp.einsum('qrgd,kgd->rgqk', queries, all_k, preferred_element_type=jnp.f...  56.6 us
    all_gather x1, waiting for transfers between devices, local_step(): all_v = lax.all_gather(local_v, 'sp', axis=0, tiled=True)  50.2 us
    dot_general x2, matrix products, decoder_layers(): jnp.dot(normed_m, w_up[layer], preferred_element_type=jnp.float32)  46.1 us
    dot_general x2, matrix products, decoder_layers(): jnp.dot(normed_m, w_gate[layer], preferred_element_type=jnp.float32)  46 us
    dot_general x2, matrix products, decoder_layers(): jnp.dot(mlp_act, w_down[layer], preferred_element_type=jnp.float32)  45.3 us
    reduce_sum x2, other arithmetic, decoder_layers(): attn_probs = jax.nn.softmax(scores, axis=-1).astype(jnp.bfloat16)  43.1 us
  transfers between devices with their start and end apart: 2, of which 2 were waited for; matrix products, arithmetic and copies ran while one was open for 16% of the time, Pallas kernels for 0%

commit v1 on v0

v1 whole, which is shorter than its diff:
```python
import functools

import jax
import jax.numpy as jnp
from jax import lax
from jax.experimental import pallas as pl
from jax.experimental.pallas import tpu as pltpu
from jax.sharding import PartitionSpec as P

NORM_EPS = 1e-6
LOG2_E = 1.4426950408889634
PIECE = 128
ROWS = 2 * PIECE
ZS = 4
SP = 2 * ZS
SEQ = SP * ROWS
HEAD_DIM = 96
HEADS_STEP = 4
LANES_STEP = HEADS_STEP * HEAD_DIM
TILE = 512
W_SLOTS = 8
D_SLOTS = 3
KV_COLS = 768
VMEM_LIMIT = 67_043_328
ANY = pl.BlockSpec(memory_space=pl.ANY)
VMEM = pl.BlockSpec(memory_space=pltpu.VMEM)
SMEM = pl.BlockSpec(memory_space=pltpu.SMEM)


def norm_rows(load, store, gain, rows):
    def block(i, carry):
        for part in range(4):
            at = pl.multiple_of(i * 64 + part * 16, 16)
            rows32 = load(at).astype(jnp.float32)
            inv_rms = lax.rsqrt(jnp.mean(rows32 * rows32, axis=-1, keepdims=True) + NORM_EPS)
            store(at, (rows32 * inv_rms * gain).astype(jnp.bfloat16))
        return carry

    lax.fori_loop(0, rows // 64, block, 0)


def remote_unit(z, step):
    flip = z // 2
    near = jnp.where(flip == 1, ZS - 1 - z, z)
    src_end, half_end = step // 2 + 1, step % 2
    src_mid = jnp.where(step < 4, 2 - 2 * (step % 2), 3)
    half_mid = jnp.where(step < 4, step // 2, step % 2)
    src = jnp.where(near == 0, src_end, src_mid)
    half = jnp.where(near == 0, half_end, half_mid)
    return jnp.where(flip == 1, ZS - 1 - src, src), half


def gather_kernel(x_ref, pos_ref, g_ref, wk_ref, wv_ref, k_out, vt_out, pos_out,
                  wk_buf, wv_buf, xbuf, ubuf, kst, vst, pbuf,
                  w_sem, x_sem, out_sem, recv, send_right, send_left, send_sib, psend, precv):
    sp = lax.axis_index('sp')
    z, core = sp // 2, sp % 2
    other = 1 - core
    sib = sp + 1 - 2 * core
    chunks = wk_buf.shape[0]
    cols = wk_buf.shape[2]

    barrier = pltpu.get_barrier_semaphore()
    for hop in range(1, SP):
        pl.semaphore_signal(barrier, inc=1, device_id={'sp': (sp + hop) % SP}, device_id_type=pl.DeviceIdType.MESH)

    def x_copy(half):
        return pltpu.make_async_copy(x_ref.at[pl.ds(half * PIECE, PIECE), :], xbuf.at[core, z, half], x_sem.at[half])

    def w_copy(n, which):
        src, dst = ((wk_ref, wk_buf), (wv_ref, wv_buf))[which]
        return pltpu.make_async_copy(src.at[:, pl.ds(n * cols, cols)], dst.at[n], w_sem.at[which, n])

    for half in range(2):
        x_copy(half).start()
    for n in range(chunks):
        for which in range(2):
            w_copy(n, which).start()
    pl.semaphore_wait(barrier, SP - 1)

    def pos_send(hop):
        return pltpu.make_async_remote_copy(src_ref=pos_ref, dst_ref=pbuf.at[sp], send_sem=psend.at[hop], recv_sem=precv.at[sp],
                                            device_id={'sp': (sp + hop) % SP}, device_id_type=pl.DeviceIdType.MESH)

    def x_send(lane, src, half, sems, target):
        return pltpu.make_async_remote_copy(src_ref=xbuf.at[lane, src, half], dst_ref=xbuf.at[lane, src, half],
                                            send_sem=sems.at[src, half], recv_sem=recv.at[lane, src, half],
                                            device_id={'sp': target}, device_id_type=pl.DeviceIdType.MESH)

    def goes_right(src):
        return (src <= z) & (z < ZS - 1)

    def goes_left(src):
        return (src >= z) & (z > 0)

    def pass_on(src, half):
        @pl.when(goes_right(src))
        def _():
            x_send(core, src, half, send_right, sp + 2).start()

        @pl.when(goes_left(src))
        def _():
            x_send(core, src, half, send_left, sp - 2).start()

        x_send(core, src, half, send_sib, sib).start()

    for half in range(2):
        x_copy(half).wait()
        pass_on(z, half)
    for hop in range(1, SP):
        pos_send(hop).start()

    gain = g_ref[...].astype(jnp.float32)

    def arrive(step):
        src, half = remote_unit(z, step)
        x_send(core, src, half, send_sib, sib).wait_recv()
        pass_on(src, half)

    middle = (z > 0) & (z < ZS - 1)

    def out_copies(par, n, src, half):
        copies = []
        for lane in range(2):
            slot = (2 * src + lane) * 2 + half
            col = pl.multiple_of(n * cols, 128)
            copies.append(pltpu.make_async_copy(kst.at[par, pl.ds(lane * PIECE, PIECE), :], k_out.at[slot, :, pl.ds(col, cols)], out_sem.at[par, lane]))
            copies.append(pltpu.make_async_copy(vst.at[par, :, pl.ds(lane * PIECE, PIECE)],
                                                vt_out.at[pl.ds(col, cols), pl.ds(pl.multiple_of(slot * PIECE, PIECE), PIECE)], out_sem.at[par, 2 + lane]))
        return copies

    def unit_step(unit, carry):
        more = (unit >= 1) & (unit < 7)

        @pl.when(more & middle)
        def _():
            arrive(unit - 1)

        far_src, far_half = remote_unit(z, jnp.maximum(unit - 2, 0))
        src = jnp.where(unit < 2, z, far_src)
        half = jnp.where(unit < 2, unit, far_half)
        x_send(other, src, half, send_sib, sib).wait_recv()
        for lane in range(2):
            def load(at, lane=lane):
                return xbuf[lane, src, half, pl.ds(at, 16), :]

            def store(at, value, lane=lane):
                ubuf[pl.ds(lane * PIECE + at, 16), :] = value

            norm_rows(load, store, gain, PIECE)

        def chunk_step(n, carry):
            par = (unit * chunks + n) % 2

            @pl.when(unit == 0)
            def _():
                w_copy(n, 0).wait()
                w_copy(n, 1).wait()

            @pl.when(unit * chunks + n >= 2)
            def _():
                for copy in out_copies(par, n, src, half):
                    copy.wait()

            keys = jnp.dot(ubuf[...], wk_buf[n], preferred_element_type=jnp.float32).astype(jnp.bfloat16)
            kst[par] = keys
            values = jnp.dot(ubuf[...], wv_buf[n], preferred_element_type=jnp.float32).astype(jnp.bfloat16)
            vst[par] = values.T
            for copy in out_copies(par, n, src, half):
                copy.start()
            return carry

        lax.fori_loop(0, chunks, chunk_step, 0)

        @pl.when(more & jnp.logical_not(middle))
        def _():
            arrive(unit - 1)

        return carry

    lax.fori_loop(0, 8, unit_step, 0)

    for par in range(2):
        for copy in out_copies(par, 0, 0, 0):
            copy.wait()

    for hop in range(1, SP):
        pos_send(hop).wait_send()
        src = (sp + hop) % SP
        pltpu.make_async_remote_copy(src_ref=pos_ref, dst_ref=pbuf.at[src], send_sem=psend.at[hop], recv_sem=precv.at[src],
                                     device_id={'sp': src}, device_id_type=pl.DeviceIdType.MESH).wait_recv()
    pbuf[sp] = pos_ref[...]
    pos_out[...] = pbuf[...]
    for src in range(ZS):
        for half in range(2):
            @pl.when(goes_right(src))
            def _(src=src, half=half):
                x_send(core, src, half, send_right, sp + 2).wait_send()

            @pl.when(goes_left(src))
            def _(src=src, half=half):
                x_send(core, src, half, send_left, sp - 2).wait_send()

            x_send(core, src, half, send_sib, sib).wait_send()


def gather_kv(rows_in, pos_rows, g_kv, w_k, w_v):
    width = rows_in.shape[1]
    out_width = w_k.shape[1]
    cols = min(KV_COLS, out_width)
    chunks = out_width // cols
    pos_tile = jnp.broadcast_to(pos_rows.reshape(2, 1, PIECE), (2, 4, PIECE)).reshape(8, PIECE)
    return pl.pallas_call(
        gather_kernel,
        out_shape=(jax.ShapeDtypeStruct((2 * SP, PIECE, out_width), jnp.bfloat16),
                   jax.ShapeDtypeStruct((out_width, SEQ), jnp.bfloat16),
                   jax.ShapeDtypeStruct((SP, 8, PIECE), jnp.int32)),
        in_specs=[ANY, VMEM, VMEM, ANY, ANY],
        out_specs=(ANY, ANY, VMEM),
        scratch_shapes=[
            pltpu.VMEM((chunks, width, cols), jnp.bfloat16),
            pltpu.VMEM((chunks, width, cols), jnp.bfloat16),
            pltpu.VMEM((2, ZS, 2, PIECE, width), jnp.bfloat16),
            pltpu.VMEM((ROWS, width), jnp.bfloat16),
            pltpu.VMEM((2, ROWS, cols), jnp.bfloat16),
            pltpu.VMEM((2, cols, ROWS), jnp.bfloat16),
            pltpu.VMEM((SP, 8, PIECE), jnp.int32),
            pltpu.SemaphoreType.DMA((2, chunks)),
            pltpu.SemaphoreType.DMA((2,)),
            pltpu.SemaphoreType.DMA((2, 4)),
            pltpu.SemaphoreType.DMA((2, ZS, 2)),
            pltpu.SemaphoreType.DMA((ZS, 2)),
            pltpu.SemaphoreType.DMA((ZS, 2)),
            pltpu.SemaphoreType.DMA((ZS, 2)),
            pltpu.SemaphoreType.DMA((SP,)),
            pltpu.SemaphoreType.DMA((SP,)),
        ],
        compiler_params=pltpu.CompilerParams(collective_id=0, has_side_effects=True, vmem_limit_bytes=VMEM_LIMIT),
        name='gather_kv',
    )(rows_in, pos_tile, g_kv.reshape(1, width), w_k, w_v)


def layers_kernel(pos_all, qpos_ref, x_ref, k_ref, vt_ref, ga_ref, gm_ref, wq_ref, wo_ref, wg_ref, wu_ref, wd_ref, h_ref,
                  wbuf, dbuf, kbuf, vbuf, qbuf, ubuf, acc, act, where_piece, w_sem, d_sem, kv_sem):
    layers, width, q_width = wq_ref.shape
    ff = wg_ref.shape[2]
    q_tiles, o_tiles, f_tiles = q_width // TILE, width // TILE, ff // TILE
    groups = q_width // LANES_STEP
    o_base = q_tiles
    f_base = q_tiles + o_tiles
    per_layer = f_base + 2 * f_tiles
    w_total, d_total = layers * per_layer, layers * f_tiles
    scale = HEAD_DIM ** -0.5 * LOG2_E

    for slot in range(2 * SP):
        where_piece[pos_all[slot // 2, 4 * (slot % 2), 0] // PIECE] = slot

    def w_src(layer, ref, tile):
        return ref.at[layer, :, pl.ds(pl.multiple_of(tile * TILE, TILE), TILE)]

    def issue_w(s):
        layer, r = s // per_layer, s % per_layer
        slot = s % W_SLOTS

        def go(ref, tile):
            pltpu.make_async_copy(w_src(layer, ref, tile), wbuf.at[slot], w_sem.at[slot]).start()

        pl.when((s < w_total) & (r < o_base))(lambda: go(wq_ref, r))
        pl.when((s < w_total) & (r >= o_base) & (r < f_base))(lambda: go(wo_ref, r - o_base))
        rr = r - f_base
        pl.when((s < w_total) & (r >= f_base) & (rr % 2 == 0))(lambda: go(wg_ref, rr // 2))
        pl.when((s < w_total) & (r >= f_base) & (rr % 2 == 1))(lambda: go(wu_ref, rr // 2))

    def wait_w(s):
        slot = s % W_SLOTS
        pltpu.make_async_copy(w_src(0, wq_ref, 0), wbuf.at[slot], w_sem.at[slot]).wait()
        return slot

    def issue_d(s):
        layer, tile = s // f_tiles, s % f_tiles
        slot = s % D_SLOTS

        @pl.when(s < d_total)
        def _():
            pltpu.make_async_copy(wd_ref.at[layer, pl.ds(pl.multiple_of(tile * TILE, TILE), TILE), :], dbuf.at[slot], d_sem.at[slot]).start()

    def wait_d(s):
        slot = s % D_SLOTS
        pltpu.make_async_copy(wd_ref.at[0, pl.ds(0, TILE), :], dbuf.at[slot], d_sem.at[slot]).wait()
        return slot

    def issue_kv(group):
        par = group % 2
        lane = pl.multiple_of(group * LANES_STEP, 128)
        for piece in range(2 * SP):
            slot = where_piece[piece]
            pltpu.make_async_copy(k_ref.at[slot, :, pl.ds(lane, LANES_STEP)], kbuf.at[par, pl.ds(piece * PIECE, PIECE), :], kv_sem.at[par, 0]).start()
            pltpu.make_async_copy(vt_ref.at[pl.ds(lane, LANES_STEP), pl.ds(pl.multiple_of(slot * PIECE, PIECE), PIECE)],
                                  vbuf.at[par, :, pl.ds(piece * PIECE, PIECE)], kv_sem.at[par, 1]).start()

    def wait_kv(group):
        par = group % 2
        pltpu.make_async_copy(kbuf.at[par], kbuf.at[par], kv_sem.at[par, 0]).wait()
        pltpu.make_async_copy(vbuf.at[par], vbuf.at[par], kv_sem.at[par, 1]).wait()
        return par

    for s in range(q_tiles):
        issue_w(s)
    issue_kv(0)
    for s in range(q_tiles, W_SLOTS):
        issue_w(s)
    for s in range(D_SLOTS):
        issue_d(s)
    h_ref[...] = x_ref[...]

    def load_h(at):
        return h_ref[pl.ds(at, 16), :]

    def store_u(at, value):
        ubuf[pl.ds(at, 16), :] = value

    def cols_of(i):
        return pl.ds(pl.multiple_of(i * TILE, TILE), TILE)

    half_keys = SEQ // 2

    def attend_group(group, carry):
        @pl.when(group + 1 < groups)
        def _():
            issue_kv(group + 1)

        par = wait_kv(group)
        lane = pl.ds(pl.multiple_of(group * LANES_STEP, 128), LANES_STEP)
        q_t = qbuf[:, lane].T
        q_low, q_high = qpos_ref[:, 0:PIECE], qpos_ref[:, PIECE:ROWS]
        rows_of = lax.broadcasted_iota(jnp.int32, (ROWS, ROWS), 0)
        key_pos = lax.broadcasted_iota(jnp.int32, (half_keys, PIECE), 0)
        see_low = key_pos <= q_low
        see_high = key_pos + half_keys <= q_high
        outs = []
        for head in range(HEADS_STEP):
            base = 0 if head < 2 else 128
            start = head * HEAD_DIM - base
            q_head = jnp.where((rows_of >= start) & (rows_of < start + HEAD_DIM), q_t[base:base + ROWS], jnp.zeros((), jnp.bfloat16))
            s_lower = jnp.dot(kbuf[par, 0:half_keys, base:base + ROWS], q_head, preferred_element_type=jnp.float32)
            s_upper = jnp.dot(kbuf[par, half_keys:SEQ, base:base + ROWS], q_head[:, PIECE:], preferred_element_type=jnp.float32)
            s_a = jnp.where(see_low, s_lower[:, :PIECE], -jnp.inf)
            s_b = s_lower[:, PIECE:]
            s_c = jnp.where(see_high, s_upper, -jnp.inf)
            m_a = jnp.max(s_a, axis=0, keepdims=True)
            m_b = jnp.maximum(jnp.max(s_b, axis=0, keepdims=True), jnp.max(s_c, axis=0, keepdims=True))
            e_a = jnp.exp2((s_a - m_a) * scale)
            e_b = jnp.exp2((s_b - m_b) * scale)
            e_c = jnp.exp2((s_c - m_b) * scale)
            l_a = 1.0 / jnp.sum(e_a, axis=0, keepdims=True)
            l_b = 1.0 / (jnp.sum(e_b, axis=0, keepdims=True) + jnp.sum(e_c, axis=0, keepdims=True))
            p_lower = jnp.concatenate([(e_a * l_a).astype(jnp.bfloat16), (e_b * l_b).astype(jnp.bfloat16)], axis=1)
            p_upper = (e_c * l_b).astype(jnp.bfloat16)
            v_t = vbuf[par, head * HEAD_DIM:(head + 1) * HEAD_DIM, :]
            o_lower = jnp.dot(v_t[:, :half_keys], p_lower, preferred_element_type=jnp.float32)
            o_upper = jnp.dot(v_t[:, half_keys:], p_upper, preferred_element_type=jnp.float32)
            outs.append(jnp.concatenate([o_lower[:, :PIECE], o_lower[:, PIECE:] + o_upper], axis=1).astype(jnp.bfloat16))
        qbuf[:, lane] = jnp.concatenate(outs, axis=0).T
        return carry

    def layer_step(layer, carry):
        w0, d0 = layer * per_layer, layer * f_tiles
        norm_rows(load_h, store_u, ga_ref[layer].astype(jnp.float32), ROWS)

        def q_step(i, carry):
            slot = wait_w(w0 + i)
            qbuf[:, cols_of(i)] = jnp.dot(ubuf[...], wbuf[slot], preferred_element_type=jnp.float32).astype(jnp.bfloat16)
            issue_w(w0 + i + W_SLOTS)
            return carry

        lax.fori_loop(0, q_tiles, q_step, 0)
        lax.fori_loop(0, groups, attend_group, 0)

        @pl.when(layer + 1 < layers)
        def _():
            issue_kv(0)

        def o_step(i, carry):
            slot = wait_w(w0 + o_base + i)
            proj = jnp.dot(qbuf[...], wbuf[slot], preferred_element_type=jnp.float32).astype(jnp.bfloat16)
            h_ref[:, cols_of(i)] = (h_ref[:, cols_of(i)].astype(jnp.float32) + proj.astype(jnp.float32)).astype(jnp.bfloat16)
            issue_w(w0 + o_base + i + W_SLOTS)
            return carry

        lax.fori_loop(0, o_tiles, o_step, 0)
        norm_rows(load_h, store_u, gm_ref[layer].astype(jnp.float32), ROWS)
        acc[...] = jnp.zeros_like(acc)

        def up_tiles(f):
            s = w0 + f_base + 2 * f
            slot_g, slot_u = wait_w(s), wait_w(s + 1)
            gate = jnp.dot(ubuf[...], wbuf[slot_g], preferred_element_type=jnp.float32).astype(jnp.bfloat16)
            upper = jnp.dot(ubuf[...], wbuf[slot_u], preferred_element_type=jnp.float32).astype(jnp.bfloat16)
            act[f % 2] = (jax.nn.silu(gate.astype(jnp.float32)) * upper.astype(jnp.float32)).astype(jnp.bfloat16)

        def up_done(f):
            s = w0 + f_base + 2 * f
            issue_w(s + W_SLOTS)
            issue_w(s + 1 + W_SLOTS)

        def down_tile(f, slot):
            acc[...] += jnp.dot(act[f % 2], dbuf[slot], preferred_element_type=jnp.float32)

        up_tiles(0)
        up_done(0)

        def f_step(f, carry):
            slot = wait_d(d0 + f - 1)
            up_tiles(f)
            down_tile(f - 1, slot)
            up_done(f)
            issue_d(d0 + f - 1 + D_SLOTS)
            return carry

        lax.fori_loop(1, f_tiles, f_step, 0)
        last = f_tiles - 1
        slot = wait_d(d0 + last)
        down_tile(last, slot)
        issue_d(d0 + last + D_SLOTS)
        h_ref[...] = (h_ref[...].astype(jnp.float32) + acc[...].astype(jnp.bfloat16).astype(jnp.float32)).astype(jnp.bfloat16)
        return carry

    lax.fori_loop(0, layers, layer_step, 0)


def decoder_layers(rows_in, pos_rows, pos_all, all_k, all_vt, g_attn, w_q, w_o, g_mlp, w_gate, w_up, w_down):
    width = rows_in.shape[1]
    q_width = w_q.shape[2]
    layers = w_q.shape[0]
    return pl.pallas_call(
        layers_kernel,
        out_shape=jax.ShapeDtypeStruct((ROWS, width), jnp.bfloat16),
        in_specs=[SMEM, VMEM, VMEM, ANY, ANY, VMEM, VMEM, ANY, ANY, ANY, ANY, ANY],
        out_specs=VMEM,
        scratch_shapes=[
            pltpu.VMEM((W_SLOTS, width, TILE), jnp.bfloat16),
            pltpu.VMEM((D_SLOTS, TILE, width), jnp.bfloat16),
            pltpu.VMEM((2, SEQ, LANES_STEP), jnp.bfloat16),
            pltpu.VMEM((2, LANES_STEP, SEQ), jnp.bfloat16),
            pltpu.VMEM((ROWS, q_width), jnp.bfloat16),
            pltpu.VMEM((ROWS, width), jnp.bfloat16),
            pltpu.VMEM((ROWS, width), jnp.float32),
            pltpu.VMEM((2, ROWS, TILE), jnp.bfloat16),
            pltpu.SMEM((2 * SP,), jnp.int32),
            pltpu.SemaphoreType.DMA((W_SLOTS,)),
            pltpu.SemaphoreType.DMA((D_SLOTS,)),
            pltpu.SemaphoreType.DMA((2, 2)),
        ],
        compiler_params=pltpu.CompilerParams(vmem_limit_bytes=VMEM_LIMIT),
        name='layers',
    )(pos_all, pos_rows.reshape(1, ROWS), rows_in, all_k, all_vt, g_attn.reshape(layers, 1, width), g_mlp.reshape(layers, 1, width), w_q, w_o.reshape(layers, q_width, width), w_gate, w_up, w_down)


def solution(mesh):
    row_spec = P(('dp', 'sp'), None)
    pos_spec = P(('dp', 'sp'))
    full = P()

    def local_step(rows_in, pos_rows, g_kv, w_k, w_v, g_attn, w_q, w_o, g_mlp, w_gate, w_up, w_down):
        all_k, all_vt, pos_all = gather_kv(rows_in, pos_rows, g_kv, w_k, w_v)
        return decoder_layers(rows_in, pos_rows, pos_all, all_k, all_vt, g_attn, w_q, w_o, g_mlp, w_gate, w_up, w_down)

    return jax.shard_map(local_step, mesh=mesh, in_specs=(row_spec, pos_spec, full, full, full, full, full, full, full, full, full, full), out_specs=row_spec, check_vma=False)
```

time: 569 us -> 324 us (0.57)
  matrix products: 318 us -> 0 us
  Pallas kernels: 0 us -> 317 us
  waiting for transfers between devices: 131 us -> 0 us
  other arithmetic: 47.4 us -> 0 us
  local copies, waits for them, and re-layouts: 38 us -> 5.25 us
  blocking collectives: 14.1 us -> 0 us
  between operations: 14 us -> 0.17 us
    dot_general x16 -> x0, matrix products: 318 us -> none  [the longest x2 59.7 us: decoder_layers(): jnp.einsum('rgqk,kgd->qrgd', attn_probs, all_v, preferred_element_type=jn...]
    pallas_call x0 -> x2, Pallas kernels: none -> 317 us  [the longest x1 187 us: decoder_layers(): pl.pallas_call(layers_kernel, out_shape=jax.ShapeDtypeStruct((ROWS, width...]
    all_gather x2 -> x0, waiting for transfers between devices: 131 us -> none  [the longest x1 81.2 us: local_step(): all_k = lax.all_gather(local_k, 'sp', axis=0, tiled=True)]
    reduce_sum x3 -> x0, other arithmetic: 44.9 us -> none  [the longest x2 43.1 us: decoder_layers(): attn_probs = jax.nn.softmax(scores, axis=-1).astype(jnp.bfloat16)]
    all_gather x2 -> x0, local copies, waits for them, and re-layouts: 33.4 us -> none  [the longest x1 16.7 us: local_step(): all_v = lax.all_gather(local_v, 'sp', axis=0, tiled=True)]
    all_gather x1 -> x0, blocking collectives: 14.1 us -> none  [local_step(): all_pos = lax.all_gather(pos_rows, 'sp', axis=0, tiled=True)]
  transfers between devices with their start and end apart: 2 -> 0, of which waited for: 2 -> 0; matrix products, arithmetic and copies ran while one was open for 16% -> 0% of each run, Pallas kernels for 0% -> 0%
where the time goes in v1:
time: 324 us; the launch traced here: 323 us
  Pallas kernels  317 us (98%)
  local copies, waits for them, and re-layouts  5.25 us (2%)
    pallas_call x1, Pallas kernels, decoder_layers(): pl.pallas_call(layers_kernel, out_shape=jax.ShapeDtypeStruct((ROWS, width...  187 us
    pallas_call x1, Pallas kernels, gather_kv(): pl.pallas_call(gather_kernel, out_shape=(jax.ShapeDtypeStruct((2 * SP, PI...  130 us

profile of v1, /device:TPU:0, one launch (start us, length us, event | category | flops | bytes accessed | tf_op | source)
XLA Modules:
  0.0 322.7 jit_solution(5625523409074761253)
XLA Ops:
  0.0 1.3 broadcast_in_dim.8
  1.3 1.3 reshape.21.g_ref
  2.6 1.3 copy.13.ga_ref
  3.9 1.3 copy.14.gm_ref
  5.3 130.3 %gather_kv.1 = (bf16[16,128,3072]{2,1,0:T(8,128)(2,1)}, bf16[3072,2048]{1,0:T(8,128)(2,1)}, s32[8,8,128]{2,1,0:T(8,128)}) custom-call(bf16[256,3072]{1,0:T(8,128)(2,1)} %x_ref.3, s32[8,128]{1,0:T(8,128)} %bitcast.7, bf16[1,3072]{1,0:T(2,128)(2,1)} %reshape.21.g_ref, bf16[3072,3072]{1,0:T(8,128)(2,1)} %wk_ref.1, bf16[3072,3072]{1,0:T(8,128)(2,1)} %wv_ref.1), custom_call_target="tpu_custom_call" | custom-call | tf_op jit(solution)/shard_map/gather_kv/pallas_call | solution.py:213
  135.5 187.0 %layers.1 = bf16[256,3072]{1,0:T(8,128)(2,1)} custom-call(s32[8,8,128]{2,1,0:T(8,128)} %get-tuple-element.8.pos_all, s32[1,256]{1,0:T(1,128)} %bitcast.11, bf16[256,3072]{1,0:T(8,128)(2,1)} %x_ref.3, bf16[16,128,3072]{2,1,0:T(8,128)(2,1)} %get-tuple-element.9.k_ref, bf16[3072,2048]{1,0:T(8,128)(2,1)} %get-tuple-element.10.vt_ref, ...), custom_call_target="tpu_custom_call" | custom-call | tf_op jit(solution)/shard_map/layers/pallas_call | solution.py:435

commit v2 on v1

--- a/solution.py
+++ b/solution.py
@@ -18,9 +18,10 @@
 HEADS_STEP = 4
 LANES_STEP = HEADS_STEP * HEAD_DIM
 TILE = 512
-W_SLOTS = 8
+W_SLOTS = 7
 D_SLOTS = 3
 KV_COLS = 768
+Q_COLS = 384
 VMEM_LIMIT = 67_043_328
 ANY = pl.BlockSpec(memory_space=pl.ANY)
 VMEM = pl.BlockSpec(memory_space=pltpu.VMEM)
@@ -50,9 +51,9 @@
     return jnp.where(flip == 1, ZS - 1 - src, src), half
 
 
-def gather_kernel(x_ref, pos_ref, g_ref, wk_ref, wv_ref, k_out, vt_out, pos_out,
-                  wk_buf, wv_buf, xbuf, ubuf, kst, vst, pbuf,
-                  w_sem, x_sem, out_sem, recv, send_right, send_left, send_sib, psend, precv):
+def gather_kernel(x_ref, pos_ref, g_ref, wk_ref, wv_ref, ga_ref, wq_ref, k_out, vt_out, pos_out, q_out,
+                  wk_buf, wv_buf, xbuf, ubuf, kst, vst, pbuf, wq_buf, qst,
+                  w_sem, x_sem, out_sem, wq_sem, qst_sem, recv, send_right, send_left, send_sib, psend, precv):
     sp = lax.axis_index('sp')
     z, core = sp // 2, sp % 2
     other = 1 - core
@@ -110,7 +111,7 @@
     for hop in range(1, SP):
         pos_send(hop).start()
 
-    gain = g_ref[...].astype(jnp.float32)
+    gain = g_ref[...].astype(jnp.float32).reshape(1, -1)
 
     def arrive(step):
         src, half = remote_unit(z, step)
@@ -178,8 +179,47 @@
 
         return carry
 
-    lax.fori_loop(0, 8, unit_step, 0)
-
+    def q_copy(i):
+        return pltpu.make_async_copy(wq_ref.at[0, :, pl.ds(pl.multiple_of(i * Q_COLS, 128), Q_COLS)], wq_buf.at[i % 2], wq_sem.at[i % 2])
+
+    def q_store(i):
+        return pltpu.make_async_copy(qst.at[i % 2], q_out.at[:, pl.ds(pl.multiple_of(i * Q_COLS, 128), Q_COLS)], qst_sem.at[i % 2])
+
+    q_steps = q_out.shape[1] // Q_COLS
+
+    def q_step(i, carry):
+        q_copy(i).wait()
+
+        @pl.when(i >= 2)
+        def _():
+            q_store(i).wait()
+
+        qst[i % 2] = jnp.dot(ubuf[...], wq_buf[i % 2], preferred_element_type=jnp.float32).astype(jnp.bfloat16)
+        q_store(i).start()
+
+        @pl.when(i + 2 < q_steps)
+        def _():
+            q_copy(i + 2).start()
+
+        return carry
+
+    for i in range(2):
+        q_copy(i).start()
+    lax.fori_loop(0, 2, unit_step, 0)
+    gain_q = ga_ref[...].astype(jnp.float32)[0:1]
+    for half in range(2):
+        def load(at, half=half):
+            return xbuf[core, z, half, pl.ds(at, 16), :]
+
+        def store(at, value, half=half):
+            ubuf[pl.ds(half * PIECE + at, 16), :] = value
+
+        norm_rows(load, store, gain_q, PIECE)
+    lax.fori_loop(0, q_steps, q_step, 0)
+    lax.fori_loop(2, 8, unit_step, 0)
+
+    for i in range(2):
+        q_store(i).wait()
     for par in range(2):
         for copy in out_copies(par, 0, 0, 0):
             copy.wait()
@@ -204,7 +244,7 @@
             x_send(core, src, half, send_sib, sib).wait_send()
 
 
-def gather_kv(rows_in, pos_rows, g_kv, w_k, w_v):
+def gather_kv(rows_in, pos_rows, g_kv, w_k, w_v, g_attn, w_q):
     width = rows_in.shape[1]
     out_width = w_k.shape[1]
     cols = min(KV_COLS, out_width)
@@ -214,9 +254,10 @@
         gather_kernel,
         out_shape=(jax.ShapeDtypeStruct((2 * SP, PIECE, out_width), jnp.bfloat16),
                    jax.ShapeDtypeStruct((out_width, SEQ), jnp.bfloat16),
-                   jax.ShapeDtypeStruct((SP, 8, PIECE), jnp.int32)),
-        in_specs=[ANY, VMEM, VMEM, ANY, ANY],
-        out_specs=(ANY, ANY, VMEM),
+                   jax.ShapeDtypeStruct((SP, 8, PIECE), jnp.int32),
+                   jax.ShapeDtypeStruct((ROWS, w_q.shape[2]), jnp.bfloat16)),
+        in_specs=[ANY, VMEM, VMEM, ANY, ANY, VMEM, ANY],
+        out_specs=(ANY, ANY, VMEM, ANY),
         scratch_shapes=[
             pltpu.VMEM((chunks, width, cols), jnp.bfloat16),
             pltpu.VMEM((chunks, width, cols), jnp.bfloat16),
@@ -225,9 +266,13 @@
             pltpu.VMEM((2, ROWS, cols), jnp.bfloat16),
             pltpu.VMEM((2, cols, ROWS), jnp.bfloat16),
             pltpu.VMEM((SP, 8, PIECE), jnp.int32),
+            pltpu.VMEM((2, width, Q_COLS), jnp.bfloat16),
+            pltpu.VMEM((2, ROWS, Q_COLS), jnp.bfloat16),
             pltpu.SemaphoreType.DMA((2, chunks)),
             pltpu.SemaphoreType.DMA((2,)),
             pltpu.SemaphoreType.DMA((2, 4)),
+            pltpu.SemaphoreType.DMA((2,)),
+            pltpu.SemaphoreType.DMA((2,)),
             pltpu.SemaphoreType.DMA((2, ZS, 2)),
             pltpu.SemaphoreType.DMA((ZS, 2)),
             pltpu.SemaphoreType.DMA((ZS, 2)),
@@ -237,11 +282,11 @@
         ],
         compiler_params=pltpu.CompilerParams(collective_id=0, has_side_effects=True, vmem_limit_bytes=VMEM_LIMIT),
         name='gather_kv',
-    )(rows_in, pos_tile, g_kv.reshape(1, width), w_k, w_v)
-
-
-def layers_kernel(pos_all, qpos_ref, x_ref, k_ref, vt_ref, ga_ref, gm_ref, wq_ref, wo_ref, wg_ref, wu_ref, wd_ref, h_ref,
-                  wbuf, dbuf, kbuf, vbuf, qbuf, ubuf, acc, act, where_piece, w_sem, d_sem, kv_sem):
+    )(rows_in, pos_tile, g_kv, w_k, w_v, g_attn, w_q)
+
+
+def layers_kernel(pos_all, qpos_ref, x_ref, k_ref, vt_ref, ga_ref, gm_ref, wq_ref, wo_ref, wg_ref, wu_ref, wd_ref, q0_ref, h_ref,
+                  wbuf, dbuf, kbuf, vbuf, qbuf, ubuf, acc, act, hide, s_low, s_up, s_max, where_piece, w_sem, d_sem, k_sem, v_sem, h_sem):
     layers, width, q_width = wq_ref.shape
     ff = wg_ref.shape[2]
     q_tiles, o_tiles, f_tiles = q_width // TILE, width // TILE, ff // TILE
@@ -249,7 +294,7 @@
     o_base = q_tiles
     f_base = q_tiles + o_tiles
     per_layer = f_base + 2 * f_tiles
-    w_total, d_total = layers * per_layer, layers * f_tiles
+    w_first, w_total, d_total = q_tiles, layers * per_layer, layers * f_tiles
     scale = HEAD_DIM ** -0.5 * LOG2_E
 
     for slot in range(2 * SP):
@@ -289,29 +334,38 @@
         pltpu.make_async_copy(wd_ref.at[0, pl.ds(0, TILE), :], dbuf.at[slot], d_sem.at[slot]).wait()
         return slot
 
-    def issue_kv(group):
-        par = group % 2
-        lane = pl.multiple_of(group * LANES_STEP, 128)
+    def issue_k(turn):
+        lane = pl.multiple_of(turn % groups * LANES_STEP, 128)
+        buf = turn % 3
         for piece in range(2 * SP):
-            slot = where_piece[piece]
-            pltpu.make_async_copy(k_ref.at[slot, :, pl.ds(lane, LANES_STEP)], kbuf.at[par, pl.ds(piece * PIECE, PIECE), :], kv_sem.at[par, 0]).start()
-            pltpu.make_async_copy(vt_ref.at[pl.ds(lane, LANES_STEP), pl.ds(pl.multiple_of(slot * PIECE, PIECE), PIECE)],
-                                  vbuf.at[par, :, pl.ds(piece * PIECE, PIECE)], kv_sem.at[par, 1]).start()
-
-    def wait_kv(group):
-        par = group % 2
-        pltpu.make_async_copy(kbuf.at[par], kbuf.at[par], kv_sem.at[par, 0]).wait()
-        pltpu.make_async_copy(vbuf.at[par], vbuf.at[par], kv_sem.at[par, 1]).wait()
-        return par
-
-    for s in range(q_tiles):
-        issue_w(s)
-    issue_kv(0)
-    for s in range(q_tiles, W_SLOTS):
+            pltpu.make_async_copy(k_ref.at[where_piece[piece], :, pl.ds(lane, LANES_STEP)], kbuf.at[buf, pl.ds(piece * PIECE, PIECE), :], k_sem.at[buf]).start()
+
+    def issue_v(turn):
+        lane = pl.multiple_of(turn % groups * LANES_STEP, 128)
+        buf = turn % 2
+        for piece in range(2 * SP):
+            col = pl.multiple_of(where_piece[piece] * PIECE, PIECE)
+            pltpu.make_async_copy(vt_ref.at[pl.ds(lane, LANES_STEP), pl.ds(col, PIECE)], vbuf.at[buf, :, pl.ds(piece * PIECE, PIECE)], v_sem.at[buf]).start()
+
+    def wait_k(turn):
+        buf = turn % 3
+        pltpu.make_async_copy(kbuf.at[buf], kbuf.at[buf], k_sem.at[buf]).wait()
+
+    def wait_v(turn):
+        buf = turn % 2
+        pltpu.make_async_copy(vbuf.at[buf], vbuf.at[buf], v_sem.at[buf]).wait()
+
+    issue_k(0)
+    issue_v(0)
+    issue_k(1)
+    for s in range(w_first, w_first + W_SLOTS):
         issue_w(s)
     for s in range(D_SLOTS):
         issue_d(s)
-    h_ref[...] = x_ref[...]
+    load_q = pltpu.make_async_copy(q0_ref, qbuf, h_sem.at[0])
+    load_x = pltpu.make_async_copy(x_ref, h_ref, h_sem.at[1])
+    load_q.start()
+    load_x.start()
 
     def load_h(at):
         return h_ref[pl.ds(at, 16), :]
@@ -319,53 +373,87 @@
     def store_u(at, value):
         ubuf[pl.ds(at, 16), :] = value
 
+    def gain_of(ref, layer):
+        gains = ref[...].astype(jnp.float32)
+        gain = gains[0:1]
+        for other in range(1, layers):
+            gain = jnp.where(layer == other, gains[other:other + 1], gain)
+        return gain
+
     def cols_of(i):
         return pl.ds(pl.multiple_of(i * TILE, TILE), TILE)
 
     half_keys = SEQ // 2
-
-    def attend_group(group, carry):
-        @pl.when(group + 1 < groups)
-        def _():
-            issue_kv(group + 1)
-
-        par = wait_kv(group)
-        lane = pl.ds(pl.multiple_of(group * LANES_STEP, 128), LANES_STEP)
-        q_t = qbuf[:, lane].T
-        q_low, q_high = qpos_ref[:, 0:PIECE], qpos_ref[:, PIECE:ROWS]
+    key_pos = lax.broadcasted_iota(jnp.int32, (half_keys, PIECE), 0)
+    hide[0:half_keys] = jnp.where(key_pos <= qpos_ref[:, 0:PIECE], 0.0, -jnp.inf)
+    hide[half_keys:SEQ] = jnp.where(key_pos + half_keys <= qpos_ref[:, PIECE:ROWS], 0.0, -jnp.inf)
+
+    def scores(turn, pair):
+        buf = turn % 3
+        base = 128 * pair
+        window_at = pl.multiple_of(turn % groups * LANES_STEP + base, 128)
+        window = qbuf[:, pl.ds(window_at, ROWS)].T
         rows_of = lax.broadcasted_iota(jnp.int32, (ROWS, ROWS), 0)
-        key_pos = lax.broadcasted_iota(jnp.int32, (half_keys, PIECE), 0)
-        see_low = key_pos <= q_low
-        see_high = key_pos + half_keys <= q_high
-        outs = []
-        for head in range(HEADS_STEP):
-            base = 0 if head < 2 else 128
-            start = head * HEAD_DIM - base
-            q_head = jnp.where((rows_of >= start) & (rows_of < start + HEAD_DIM), q_t[base:base + ROWS], jnp.zeros((), jnp.bfloat16))
-            s_lower = jnp.dot(kbuf[par, 0:half_keys, base:base + ROWS], q_head, preferred_element_type=jnp.float32)
-            s_upper = jnp.dot(kbuf[par, half_keys:SEQ, base:base + ROWS], q_head[:, PIECE:], preferred_element_type=jnp.float32)
-            s_a = jnp.where(see_low, s_lower[:, :PIECE], -jnp.inf)
-            s_b = s_lower[:, PIECE:]
-            s_c = jnp.where(see_high, s_upper, -jnp.inf)
+        heads = []
+        for i in range(2):
+            start = HEAD_DIM * (2 * pair + i) - base
+            heads.append(jnp.where((rows_of >= start) & (rows_of < start + HEAD_DIM), window, jnp.zeros((), jnp.bfloat16)))
+        both = jnp.concatenate([heads[0][:, PIECE:], heads[1][:, PIECE:]], axis=1)
+        upper = jnp.dot(kbuf[buf, half_keys:SEQ, base:base + ROWS], both, preferred_element_type=jnp.float32)
+        for i in range(2):
+            lower = jnp.dot(kbuf[buf, 0:half_keys, base:base + ROWS], heads[i], preferred_element_type=jnp.float32)
+            s_a = lower[:, :PIECE] + hide[0:half_keys]
+            s_b = lower[:, PIECE:]
+            s_c = upper[:, i * PIECE:(i + 1) * PIECE] + hide[half_keys:SEQ]
+            s_low[pair, i, :, 0:PIECE] = s_a
+            s_low[pair, i, :, PIECE:ROWS] = s_b
+            s_up[pair, i] = s_c
             m_a = jnp.max(s_a, axis=0, keepdims=True)
             m_b = jnp.maximum(jnp.max(s_b, axis=0, keepdims=True), jnp.max(s_c, axis=0, keepdims=True))
-            e_a = jnp.exp2((s_a - m_a) * scale)
-            e_b = jnp.exp2((s_b - m_b) * scale)
-            e_c = jnp.exp2((s_c - m_b) * scale)
-            l_a = 1.0 / jnp.sum(e_a, axis=0, keepdims=True)
-            l_b = 1.0 / (jnp.sum(e_b, axis=0, keepdims=True) + jnp.sum(e_c, axis=0, keepdims=True))
-            p_lower = jnp.concatenate([(e_a * l_a).astype(jnp.bfloat16), (e_b * l_b).astype(jnp.bfloat16)], axis=1)
-            p_upper = (e_c * l_b).astype(jnp.bfloat16)
-            v_t = vbuf[par, head * HEAD_DIM:(head + 1) * HEAD_DIM, :]
-            o_lower = jnp.dot(v_t[:, :half_keys], p_lower, preferred_element_type=jnp.float32)
-            o_upper = jnp.dot(v_t[:, half_keys:], p_upper, preferred_element_type=jnp.float32)
-            outs.append(jnp.concatenate([o_lower[:, :PIECE], o_lower[:, PIECE:] + o_upper], axis=1).astype(jnp.bfloat16))
-        qbuf[:, lane] = jnp.concatenate(outs, axis=0).T
+            s_max[pair, i] = jnp.broadcast_to(jnp.concatenate([m_a, m_b], axis=1), (8, ROWS))
+
+    def attend(turn, pair):
+        buf = turn % 2
+        p_lowers, p_uppers, inverses = [], [], []
+        for i in range(2):
+            m_a, m_b = s_max[pair, i, 0:1, 0:PIECE], s_max[pair, i, 0:1, PIECE:ROWS]
+            e_a = jnp.exp2((s_low[pair, i, :, 0:PIECE] - m_a) * scale)
+            e_b = jnp.exp2((s_low[pair, i, :, PIECE:ROWS] - m_b) * scale)
+            e_c = jnp.exp2((s_up[pair, i] - m_b) * scale)
+            l_a = jnp.sum(e_a, axis=0, keepdims=True)
+            l_b = jnp.sum(e_b, axis=0, keepdims=True) + jnp.sum(e_c, axis=0, keepdims=True)
+            p_lowers.append(jnp.concatenate([e_a.astype(jnp.bfloat16), e_b.astype(jnp.bfloat16)], axis=1))
+            p_uppers.append(e_c.astype(jnp.bfloat16))
+            inverses.append(1.0 / jnp.concatenate([l_a, l_b], axis=1))
+        top = 2 * pair * HEAD_DIM
+        o_upper = jnp.dot(vbuf[buf, top:top + 2 * HEAD_DIM, half_keys:SEQ], jnp.concatenate(p_uppers, axis=1), preferred_element_type=jnp.float32)
+        outs = []
+        for i in range(2):
+            o_lower = jnp.dot(vbuf[buf, top + i * HEAD_DIM:top + (i + 1) * HEAD_DIM, 0:half_keys], p_lowers[i], preferred_element_type=jnp.float32)
+            mine = o_upper[i * HEAD_DIM:(i + 1) * HEAD_DIM, i * PIECE:(i + 1) * PIECE]
+            o_t = jnp.concatenate([o_lower[:, :PIECE], o_lower[:, PIECE:] + mine], axis=1)
+            outs.append((o_t * inverses[i]).astype(jnp.bfloat16))
+        return outs
+
+    def attend_group(turn, carry):
+        wait_k(turn + 1)
+        wait_v(turn)
+        issue_k(turn + 2)
+        issue_v(turn + 1)
+        scores(turn, 1)
+        outs = attend(turn, 0)
+        scores(turn + 1, 0)
+        outs += attend(turn, 1)
+        lane = pl.ds(pl.multiple_of(turn % groups * LANES_STEP, 128), LANES_STEP)
+        ubuf[:, lane] = jnp.concatenate(outs, axis=0).T
         return carry
+
+    load_q.wait()
+    load_x.wait()
+    wait_k(0)
 
     def layer_step(layer, carry):
         w0, d0 = layer * per_layer, layer * f_tiles
-        norm_rows(load_h, store_u, ga_ref[layer].astype(jnp.float32), ROWS)
 
         def q_step(i, carry):
             slot = wait_w(w0 + i)
@@ -373,22 +461,24 @@
             issue_w(w0 + i + W_SLOTS)
             return carry
 
-        lax.fori_loop(0, q_tiles, q_step, 0)
-        lax.fori_loop(0, groups, attend_group, 0)
-
-        @pl.when(layer + 1 < layers)
-        def _():
-            issue_kv(0)
+        @pl.when(layer > 0)
+        def _():
+            norm_rows(load_h, store_u, gain_of(ga_ref, layer), ROWS)
+            lax.fori_loop(0, q_tiles, q_step, 0)
+
+        first = layer * groups
+        scores(first, 0)
+        lax.fori_loop(first, first + groups, attend_group, 0)
 
         def o_step(i, carry):
             slot = wait_w(w0 + o_base + i)
-            proj = jnp.dot(qbuf[...], wbuf[slot], preferred_element_type=jnp.float32).astype(jnp.bfloat16)
+            proj = jnp.dot(ubuf[...], wbuf[slot], preferred_element_type=jnp.float32).astype(jnp.bfloat16)
             h_ref[:, cols_of(i)] = (h_ref[:, cols_of(i)].astype(jnp.float32) + proj.astype(jnp.float32)).astype(jnp.bfloat16)
             issue_w(w0 + o_base + i + W_SLOTS)
             return carry
 
         lax.fori_loop(0, o_tiles, o_step, 0)
-        norm_rows(load_h, store_u, gm_ref[layer].astype(jnp.float32), ROWS)
+        norm_rows(load_h, store_u, gain_of(gm_ref, layer), ROWS)
         acc[...] = jnp.zeros_like(acc)
 
         def up_tiles(f):
@@ -426,34 +516,42 @@
         return carry
 
     lax.fori_loop(0, layers, layer_step, 0)
-
-
-def decoder_layers(rows_in, pos_rows, pos_all, all_k, all_vt, g_attn, w_q, w_o, g_mlp, w_gate, w_up, w_down):
+    wait_v(layers * groups)
+    wait_k(layers * groups + 1)
+
+
+def decoder_layers(rows_in, q_first, pos_rows, pos_all, all_k, all_vt, g_attn, w_q, w_o, g_mlp, w_gate, w_up, w_down):
     width = rows_in.shape[1]
     q_width = w_q.shape[2]
     layers = w_q.shape[0]
     return pl.pallas_call(
         layers_kernel,
         out_shape=jax.ShapeDtypeStruct((ROWS, width), jnp.bfloat16),
-        in_specs=[SMEM, VMEM, VMEM, ANY, ANY, VMEM, VMEM, ANY, ANY, ANY, ANY, ANY],
+        in_specs=[SMEM, VMEM, ANY, ANY, ANY, VMEM, VMEM, ANY, ANY, ANY, ANY, ANY, ANY],
         out_specs=VMEM,
         scratch_shapes=[
             pltpu.VMEM((W_SLOTS, width, TILE), jnp.bfloat16),
             pltpu.VMEM((D_SLOTS, TILE, width), jnp.bfloat16),
-            pltpu.VMEM((2, SEQ, LANES_STEP), jnp.bfloat16),
+            pltpu.VMEM((3, SEQ, LANES_STEP), jnp.bfloat16),
             pltpu.VMEM((2, LANES_STEP, SEQ), jnp.bfloat16),
             pltpu.VMEM((ROWS, q_width), jnp.bfloat16),
             pltpu.VMEM((ROWS, width), jnp.bfloat16),
             pltpu.VMEM((ROWS, width), jnp.float32),
             pltpu.VMEM((2, ROWS, TILE), jnp.bfloat16),
+            pltpu.VMEM((SEQ, PIECE), jnp.float32),
+            pltpu.VMEM((2, 2, SEQ // 2, ROWS), jnp.float32),
+            pltpu.VMEM((2, 2, SEQ // 2, PIECE), jnp.float32),
+            pltpu.VMEM((2, 2, 8, ROWS), jnp.float32),
             pltpu.SMEM((2 * SP,), jnp.int32),
             pltpu.SemaphoreType.DMA((W_SLOTS,)),
             pltpu.SemaphoreType.DMA((D_SLOTS,)),
-            pltpu.SemaphoreType.DMA((2, 2)),
+            pltpu.SemaphoreType.DMA((3,)),
+            pltpu.SemaphoreType.DMA((2,)),
+            pltpu.SemaphoreType.DMA((2,)),
         ],
         compiler_params=pltpu.CompilerParams(vmem_limit_bytes=VMEM_LIMIT),
         name='layers',
-    )(pos_all, pos_rows.reshape(1, ROWS), rows_in, all_k, all_vt, g_attn.reshape(layers, 1, width), g_mlp.reshape(layers, 1, width), w_q, w_o.reshape(layers, q_width, width), w_gate, w_up, w_down)
+    )(pos_all, pos_rows.reshape(1, ROWS), rows_in, all_k, all_vt, g_attn, g_mlp, w_q, w_o.reshape(layers, q_width, width), w_gate, w_up, w_down, q_first)
 
 
 def solution(mesh):
@@ -462,7 +560,7 @@
     full = P()
 
     def local_step(rows_in, pos_rows, g_kv, w_k, w_v, g_attn, w_q, w_o, g_mlp, w_gate, w_up, w_down):
-        all_k, all_vt, pos_all = gather_kv(rows_in, pos_rows, g_kv, w_k, w_v)
-        return decoder_layers(rows_in, pos_rows, pos_all, all_k, all_vt, g_attn, w_q, w_o, g_mlp, w_gate, w_up, w_down)
+        all_k, all_vt, pos_all, q_first = gather_kv(rows_in, pos_rows, g_kv, w_k, w_v, g_attn, w_q)
+        return decoder_layers(rows_in, q_first, pos_rows, pos_all, all_k, all_vt, g_attn, w_q, w_o, g_mlp, w_gate, w_up, w_down)
 
     return jax.shard_map(local_step, mesh=mesh, in_specs=(row_spec, pos_spec, full, full, full, full, full, full, full, full, full, full), out_specs=row_spec, check_vma=False)

time: 324 us -> 299 us (0.923)
  Pallas kernels: 317 us -> 296 us
  local copies, waits for them, and re-layouts: 5.25 us -> 1.27 us
    pallas_call x1, Pallas kernels: 187 us -> 158 us  [decoder_layers(): pl.pallas_call(layers_kernel, out_shape=jax.ShapeDtypeStruct((ROWS, width...]
    pallas_call x1, Pallas kernels: 130 us -> 138 us  [gather_kv(): pl.pallas_call(gather_kernel, out_shape=(jax.ShapeDtypeStruct((2 * SP, PI...]
    reshape x3 -> x0, local copies, waits for them, and re-layouts: 3.98 us -> none  [the longest x1 1.35 us: decoder_layers(): g_attn.reshape(layers, 1, width)]
where the time goes in v2:
time: 299 us; the launch traced here: 298 us
  Pallas kernels  296 us (99%)
    pallas_call x1, Pallas kernels, decoder_layers(): pl.pallas_call(layers_kernel, out_shape=jax.ShapeDtypeStruct((ROWS, width...  158 us
    pallas_call x1, Pallas kernels, gather_kv(): pl.pallas_call(gather_kernel, out_shape=(jax.ShapeDtypeStruct((2 * SP, PI...  138 us

profile of v2, /device:TPU:0, one launch (start us, length us, event | category | flops | bytes accessed | tf_op | source)
XLA Modules:
  0.0 297.7 jit_solution(4307318813296733209)
XLA Ops:
  0.0 1.3 broadcast_in_dim.8
  1.3 138.3 %gather_kv.1 = (bf16[16,128,3072]{2,1,0:T(8,128)(2,1)}, bf16[3072,2048]{1,0:T(8,128)(2,1)}, s32[8,8,128]{2,1,0:T(8,128)}, bf16[256,3072]{1,0:T(8,128)(2,1)}) custom-call(bf16[256,3072]{1,0:T(8,128)(2,1)} %x_ref.3, s32[8,128]{1,0:T(8,128)} %bitcast.5, bf16[3072]{0:T(1024)(128)(2,1)} %g_ref.1, bf16[3072,3072]{1,0:T(8,128)(2,1)} %wk_ref.1, ...), custom_call_target="tpu_custom_call" | custom-call | tf_op jit(solution)/shard_map/gather_kv/pallas_call | solution.py:253
  139.5 158.0 %layers.1 = bf16[256,3072]{1,0:T(8,128)(2,1)} custom-call(s32[8,8,128]{2,1,0:T(8,128)} %get-tuple-element.9.pos_all, s32[1,256]{1,0:T(1,128)} %bitcast.7, bf16[256,3072]{1,0:T(8,128)(2,1)} %x_ref.3, bf16[16,128,3072]{2,1,0:T(8,128)(2,1)} %get-tuple-element.10.k_ref, bf16[3072,2048]{1,0:T(8,128)(2,1)} %get-tuple-element.11.vt_ref, bf16[2,3072]{1,0:T(2,128)(2,1)} %ga_ref.3, ...), custom_call_target="tpu_custom_call" | custom-call | tf_op jit(solution)/shard_map/layers/pallas_call | solution.py:527

commit v3 on v2

--- a/solution.py
+++ b/solution.py
@@ -21,7 +21,7 @@
 W_SLOTS = 7
 D_SLOTS = 3
 KV_COLS = 768
-Q_COLS = 384
+Q_COLS = 512
 VMEM_LIMIT = 67_043_328
 ANY = pl.BlockSpec(memory_space=pl.ANY)
 VMEM = pl.BlockSpec(memory_space=pltpu.VMEM)
@@ -131,11 +131,14 @@
         return copies
 
     def unit_step(unit, carry):
-        more = (unit >= 1) & (unit < 7)
-
-        @pl.when(more & middle)
-        def _():
-            arrive(unit - 1)
+        @pl.when(middle & ((unit == 1) | (unit == 2)))
+        def _():
+            arrive(2 * unit - 2)
+            arrive(2 * unit - 1)
+
+        @pl.when(middle & ((unit == 3) | (unit == 5)))
+        def _():
+            arrive(4 + unit // 5)
 
         far_src, far_half = remote_unit(z, jnp.maximum(unit - 2, 0))
         src = jnp.where(unit < 2, z, far_src)
@@ -173,7 +176,7 @@
 
         lax.fori_loop(0, chunks, chunk_step, 0)
 
-        @pl.when(more & jnp.logical_not(middle))
+        @pl.when((unit >= 1) & (unit < 7) & jnp.logical_not(middle))
         def _():
             arrive(unit - 1)
 
@@ -286,12 +289,13 @@
 
 
 def layers_kernel(pos_all, qpos_ref, x_ref, k_ref, vt_ref, ga_ref, gm_ref, wq_ref, wo_ref, wg_ref, wu_ref, wd_ref, q0_ref, h_ref,
-                  wbuf, dbuf, kbuf, vbuf, qbuf, ubuf, acc, act, hide, s_low, s_up, s_max, where_piece, w_sem, d_sem, k_sem, v_sem, h_sem):
+                  wbuf, dbuf, kbuf, vbuf, qbuf, ubuf, acc, act_new, act_old, hide, s_low, s_up, s_max, where_piece, w_sem, d_sem, k_sem, v_sem, h_sem):
     layers, width, q_width = wq_ref.shape
     ff = wg_ref.shape[2]
     q_tiles, o_tiles, f_tiles = q_width // TILE, width // TILE, ff // TILE
     groups = q_width // LANES_STEP
     o_base = q_tiles
+    q_pack, o_pack = 2 - q_tiles % 2, 2 - o_tiles % 2
     f_base = q_tiles + o_tiles
     per_layer = f_base + 2 * f_tiles
     w_first, w_total, d_total = q_tiles, layers * per_layer, layers * f_tiles
@@ -308,7 +312,7 @@
         slot = s % W_SLOTS
 
         def go(ref, tile):
-            pltpu.make_async_copy(w_src(layer, ref, tile), wbuf.at[slot], w_sem.at[slot]).start()
+            pltpu.make_async_copy(w_src(layer, ref, tile), wbuf.at[slot], w_sem.at[slot]).start(priority=1)
 
         pl.when((s < w_total) & (r < o_base))(lambda: go(wq_ref, r))
         pl.when((s < w_total) & (r >= o_base) & (r < f_base))(lambda: go(wo_ref, r - o_base))
@@ -327,7 +331,7 @@
 
         @pl.when(s < d_total)
         def _():
-            pltpu.make_async_copy(wd_ref.at[layer, pl.ds(pl.multiple_of(tile * TILE, TILE), TILE), :], dbuf.at[slot], d_sem.at[slot]).start()
+            pltpu.make_async_copy(wd_ref.at[layer, pl.ds(pl.multiple_of(tile * TILE, TILE), TILE), :], dbuf.at[slot], d_sem.at[slot]).start(priority=1)
 
     def wait_d(s):
         slot = s % D_SLOTS
@@ -455,29 +459,35 @@
     def layer_step(layer, carry):
         w0, d0 = layer * per_layer, layer * f_tiles
 
-        def q_step(i, carry):
-            slot = wait_w(w0 + i)
-            qbuf[:, cols_of(i)] = jnp.dot(ubuf[...], wbuf[slot], preferred_element_type=jnp.float32).astype(jnp.bfloat16)
-            issue_w(w0 + i + W_SLOTS)
+        def q_step(step, carry):
+            tiles = [q_pack * step + j for j in range(q_pack)]
+            slots = [wait_w(w0 + i) for i in tiles]
+            for i, slot in zip(tiles, slots):
+                qbuf[:, cols_of(i)] = jnp.dot(ubuf[...], wbuf[slot], preferred_element_type=jnp.float32).astype(jnp.bfloat16)
+            for i in tiles:
+                issue_w(w0 + i + W_SLOTS)
             return carry
 
         @pl.when(layer > 0)
         def _():
             norm_rows(load_h, store_u, gain_of(ga_ref, layer), ROWS)
-            lax.fori_loop(0, q_tiles, q_step, 0)
+            lax.fori_loop(0, q_tiles // q_pack, q_step, 0)
 
         first = layer * groups
         scores(first, 0)
         lax.fori_loop(first, first + groups, attend_group, 0)
 
-        def o_step(i, carry):
-            slot = wait_w(w0 + o_base + i)
-            proj = jnp.dot(ubuf[...], wbuf[slot], preferred_element_type=jnp.float32).astype(jnp.bfloat16)
-            h_ref[:, cols_of(i)] = (h_ref[:, cols_of(i)].astype(jnp.float32) + proj.astype(jnp.float32)).astype(jnp.bfloat16)
-            issue_w(w0 + o_base + i + W_SLOTS)
+        def o_step(step, carry):
+            tiles = [o_pack * step + j for j in range(o_pack)]
+            slots = [wait_w(w0 + o_base + i) for i in tiles]
+            for i, slot in zip(tiles, slots):
+                proj = jnp.dot(ubuf[...], wbuf[slot], preferred_element_type=jnp.float32).astype(jnp.bfloat16)
+                h_ref[:, cols_of(i)] = (h_ref[:, cols_of(i)].astype(jnp.float32) + proj.astype(jnp.float32)).astype(jnp.bfloat16)
+            for i in tiles:
+                issue_w(w0 + o_base + i + W_SLOTS)
             return carry
 
-        lax.fori_loop(0, o_tiles, o_step, 0)
+        lax.fori_loop(0, o_tiles // o_pack, o_step, 0)
         norm_rows(load_h, store_u, gain_of(gm_ref, layer), ROWS)
         acc[...] = jnp.zeros_like(acc)
 
@@ -486,23 +496,25 @@
             slot_g, slot_u = wait_w(s), wait_w(s + 1)
             gate = jnp.dot(ubuf[...], wbuf[slot_g], preferred_element_type=jnp.float32).astype(jnp.bfloat16)
             upper = jnp.dot(ubuf[...], wbuf[slot_u], preferred_element_type=jnp.float32).astype(jnp.bfloat16)
-            act[f % 2] = (jax.nn.silu(gate.astype(jnp.float32)) * upper.astype(jnp.float32)).astype(jnp.bfloat16)
+            act_new[...] = (jax.nn.silu(gate.astype(jnp.float32)) * upper.astype(jnp.float32)).astype(jnp.bfloat16)
 
         def up_done(f):
             s = w0 + f_base + 2 * f
             issue_w(s + W_SLOTS)
             issue_w(s + 1 + W_SLOTS)
 
-        def down_tile(f, slot):
-            acc[...] += jnp.dot(act[f % 2], dbuf[slot], preferred_element_type=jnp.float32)
+        def down_tile(slot):
+            acc[...] += jnp.dot(act_old[...], dbuf[slot], preferred_element_type=jnp.float32)
 
         up_tiles(0)
+        act_old[...] = act_new[...]
         up_done(0)
 
         def f_step(f, carry):
             slot = wait_d(d0 + f - 1)
             up_tiles(f)
-            down_tile(f - 1, slot)
+            down_tile(slot)
+            act_old[...] = act_new[...]
             up_done(f)
             issue_d(d0 + f - 1 + D_SLOTS)
             return carry
@@ -510,7 +522,7 @@
         lax.fori_loop(1, f_tiles, f_step, 0)
         last = f_tiles - 1
         slot = wait_d(d0 + last)
-        down_tile(last, slot)
+        down_tile(slot)
         issue_d(d0 + last + D_SLOTS)
         h_ref[...] = (h_ref[...].astype(jnp.float32) + acc[...].astype(jnp.bfloat16).astype(jnp.float32)).astype(jnp.bfloat16)
         return carry
@@ -537,7 +549,8 @@
             pltpu.VMEM((ROWS, q_width), jnp.bfloat16),
             pltpu.VMEM((ROWS, width), jnp.bfloat16),
             pltpu.VMEM((ROWS, width), jnp.float32),
-            pltpu.VMEM((2, ROWS, TILE), jnp.bfloat16),
+            pltpu.VMEM((ROWS, TILE), jnp.bfloat16),
+            pltpu.VMEM((ROWS, TILE), jnp.bfloat16),
             pltpu.VMEM((SEQ, PIECE), jnp.float32),
             pltpu.VMEM((2, 2, SEQ // 2, ROWS), jnp.float32),
             pltpu.VMEM((2, 2, SEQ // 2, PIECE), jnp.float32),

time: 299 us -> 282 us (0.943)
  Pallas kernels: 296 us -> 279 us
    pallas_call x1, Pallas kernels: 158 us -> 149 us  [decoder_layers(): pl.pallas_call(layers_kernel, out_shape=jax.ShapeDtypeStruct((ROWS, width...]
    pallas_call x1, Pallas kernels: 138 us -> 130 us  [gather_kv(): pl.pallas_call(gather_kernel, out_shape=(jax.ShapeDtypeStruct((2 * SP, PI...]
where the time goes in v3:
time: 282 us; the launch traced here: 281 us
  Pallas kernels  279 us (99%)
    pallas_call x1, Pallas kernels, decoder_layers(): pl.pallas_call(layers_kernel, out_shape=jax.ShapeDtypeStruct((ROWS, width...  149 us
    pallas_call x1, Pallas kernels, gather_kv(): pl.pallas_call(gather_kernel, out_shape=(jax.ShapeDtypeStruct((2 * SP, PI...  130 us

profile of v3, /device:TPU:0, one launch (start us, length us, event | category | flops | bytes accessed | tf_op | source)
XLA Modules:
  0.0 280.8 jit_solution(11441962655513470485)
XLA Ops:
  0.0 1.3 broadcast_in_dim.8
  1.3 130.4 %gather_kv.1 = (bf16[16,128,3072]{2,1,0:T(8,128)(2,1)}, bf16[3072,2048]{1,0:T(8,128)(2,1)}, s32[8,8,128]{2,1,0:T(8,128)}, bf16[256,3072]{1,0:T(8,128)(2,1)}) custom-call(bf16[256,3072]{1,0:T(8,128)(2,1)} %x_ref.3, s32[8,128]{1,0:T(8,128)} %bitcast.5, bf16[3072]{0:T(1024)(128)(2,1)} %g_ref.1, bf16[3072,3072]{1,0:T(8,128)(2,1)} %wk_ref.1, ...), custom_call_target="tpu_custom_call" | custom-call | tf_op jit(solution)/shard_map/gather_kv/pallas_call | solution.py:256
  131.6 149.0 %layers.1 = bf16[256,3072]{1,0:T(8,128)(2,1)} custom-call(s32[8,8,128]{2,1,0:T(8,128)} %get-tuple-element.9.pos_all, s32[1,256]{1,0:T(1,128)} %bitcast.7, bf16[256,3072]{1,0:T(8,128)(2,1)} %x_ref.3, bf16[16,128,3072]{2,1,0:T(8,128)(2,1)} %get-tuple-element.10.k_ref, bf16[3072,2048]{1,0:T(8,128)(2,1)} %get-tuple-element.11.vt_ref, bf16[2,3072]{1,0:T(2,128)(2,1)} %ga_ref.3, ...), custom_call_target="tpu_custom_call" | custom-call | tf_op jit(solution)/shard_map/layers/pallas_call | solution.py:539

commit v4 on v3

--- a/solution.py
+++ b/solution.py
@@ -53,7 +53,7 @@
 
 def gather_kernel(x_ref, pos_ref, g_ref, wk_ref, wv_ref, ga_ref, wq_ref, k_out, vt_out, pos_out, q_out,
                   wk_buf, wv_buf, xbuf, ubuf, kst, vst, pbuf, wq_buf, qst,
-                  w_sem, x_sem, out_sem, wq_sem, qst_sem, recv, send_right, send_left, send_sib, psend, precv):
+                  w_sem, x_sem, out_sem, peer_send, peer_recv, wq_sem, qst_sem, recv, send_right, send_left, send_sib, psend, precv):
     sp = lax.axis_index('sp')
     z, core = sp // 2, sp % 2
     other = 1 - core
@@ -61,6 +61,9 @@
     chunks = wk_buf.shape[0]
     cols = wk_buf.shape[2]
 
+    def cols_of(n):
+        return pl.ds(pl.multiple_of((core * chunks + n) * cols, 128), cols)
+
     barrier = pltpu.get_barrier_semaphore()
     for hop in range(1, SP):
         pl.semaphore_signal(barrier, inc=1, device_id={'sp': (sp + hop) % SP}, device_id_type=pl.DeviceIdType.MESH)
@@ -70,7 +73,7 @@
 
     def w_copy(n, which):
         src, dst = ((wk_ref, wk_buf), (wv_ref, wv_buf))[which]
-        return pltpu.make_async_copy(src.at[:, pl.ds(n * cols, cols)], dst.at[n], w_sem.at[which, n])
+        return pltpu.make_async_copy(src.at[:, cols_of(n)], dst.at[n], w_sem.at[which, n])
 
     for half in range(2):
         x_copy(half).start()
@@ -120,25 +123,41 @@
 
     middle = (z > 0) & (z < ZS - 1)
 
-    def out_copies(par, n, src, half):
-        copies = []
+    def out_copies(par, unit, n, src, half):
+        mine, theirs = [], []
         for lane in range(2):
             slot = (2 * src + lane) * 2 + half
-            col = pl.multiple_of(n * cols, 128)
-            copies.append(pltpu.make_async_copy(kst.at[par, pl.ds(lane * PIECE, PIECE), :], k_out.at[slot, :, pl.ds(col, cols)], out_sem.at[par, lane]))
-            copies.append(pltpu.make_async_copy(vst.at[par, :, pl.ds(lane * PIECE, PIECE)],
-                                                vt_out.at[pl.ds(col, cols), pl.ds(pl.multiple_of(slot * PIECE, PIECE), PIECE)], out_sem.at[par, 2 + lane]))
-        return copies
+            rows = pl.ds(lane * PIECE, PIECE)
+            pairs = ((kst.at[par, rows, :], k_out.at[slot, :, cols_of(n)]),
+                     (vst.at[par, :, rows], vt_out.at[cols_of(n), pl.ds(pl.multiple_of(slot * PIECE, PIECE), PIECE)]))
+            for which, (source, target) in enumerate(pairs):
+                j = 2 * lane + which
+                mine.append(pltpu.make_async_copy(source, target, out_sem.at[par, j]))
+                theirs.append(pltpu.make_async_remote_copy(src_ref=source, dst_ref=target, send_sem=peer_send.at[par, j], recv_sem=peer_recv.at[unit, n, j],
+                                                           device_id={'sp': sib}, device_id_type=pl.DeviceIdType.MESH))
+        return mine, theirs
+
+    def out_start(par, unit, n, src, half):
+        mine, theirs = out_copies(par, unit, n, src, half)
+        for copy in theirs + mine:
+            copy.start()
+
+    def out_wait(par):
+        mine, theirs = out_copies(par, 0, 0, 0, 0)
+        for copy in mine:
+            copy.wait()
+        for copy in theirs:
+            copy.wait_send()
 
     def unit_step(unit, carry):
-        @pl.when(middle & ((unit == 1) | (unit == 2)))
-        def _():
-            arrive(2 * unit - 2)
-            arrive(2 * unit - 1)
-
-        @pl.when(middle & ((unit == 3) | (unit == 5)))
-        def _():
-            arrive(4 + unit // 5)
+        @pl.when(middle & ((unit == 2) | (unit == 4)))
+        def _():
+            arrive(unit - 2)
+            arrive(unit - 1)
+
+        @pl.when((middle & (unit >= 6)) | (jnp.logical_not(middle) & (unit >= 2)))
+        def _():
+            arrive(unit - 2)
 
         far_src, far_half = remote_unit(z, jnp.maximum(unit - 2, 0))
         src = jnp.where(unit < 2, z, far_src)
@@ -163,22 +182,16 @@
 
             @pl.when(unit * chunks + n >= 2)
             def _():
-                for copy in out_copies(par, n, src, half):
-                    copy.wait()
+                out_wait(par)
 
             keys = jnp.dot(ubuf[...], wk_buf[n], preferred_element_type=jnp.float32).astype(jnp.bfloat16)
             kst[par] = keys
             values = jnp.dot(ubuf[...], wv_buf[n], preferred_element_type=jnp.float32).astype(jnp.bfloat16)
             vst[par] = values.T
-            for copy in out_copies(par, n, src, half):
-                copy.start()
+            out_start(par, unit, n, src, half)
             return carry
 
         lax.fori_loop(0, chunks, chunk_step, 0)
-
-        @pl.when((unit >= 1) & (unit < 7) & jnp.logical_not(middle))
-        def _():
-            arrive(unit - 1)
 
         return carry
 
@@ -224,8 +237,15 @@
     for i in range(2):
         q_store(i).wait()
     for par in range(2):
-        for copy in out_copies(par, 0, 0, 0):
-            copy.wait()
+        out_wait(par)
+
+    def peer_wait(unit, carry):
+        for n in range(chunks):
+            for copy in out_copies(0, unit, n, 0, 0)[1]:
+                copy.wait_recv()
+        return carry
+
+    lax.fori_loop(0, 8, peer_wait, 0)
 
     for hop in range(1, SP):
         pos_send(hop).wait_send()
@@ -251,13 +271,13 @@
     width = rows_in.shape[1]
     out_width = w_k.shape[1]
     cols = min(KV_COLS, out_width)
-    chunks = out_width // cols
-    pos_tile = jnp.broadcast_to(pos_rows.reshape(2, 1, PIECE), (2, 4, PIECE)).reshape(8, PIECE)
+    chunks = out_width // cols // 2
+    pos_tile = pos_rows.reshape(2, PIECE)
     return pl.pallas_call(
         gather_kernel,
         out_shape=(jax.ShapeDtypeStruct((2 * SP, PIECE, out_width), jnp.bfloat16),
                    jax.ShapeDtypeStruct((out_width, SEQ), jnp.bfloat16),
-                   jax.ShapeDtypeStruct((SP, 8, PIECE), jnp.int32),
+                   jax.ShapeDtypeStruct((SP, 2, PIECE), jnp.int32),
                    jax.ShapeDtypeStruct((ROWS, w_q.shape[2]), jnp.bfloat16)),
         in_specs=[ANY, VMEM, VMEM, ANY, ANY, VMEM, ANY],
         out_specs=(ANY, ANY, VMEM, ANY),
@@ -268,12 +288,14 @@
             pltpu.VMEM((ROWS, width), jnp.bfloat16),
             pltpu.VMEM((2, ROWS, cols), jnp.bfloat16),
             pltpu.VMEM((2, cols, ROWS), jnp.bfloat16),
-            pltpu.VMEM((SP, 8, PIECE), jnp.int32),
+            pltpu.VMEM((SP, 2, PIECE), jnp.int32),
             pltpu.VMEM((2, width, Q_COLS), jnp.bfloat16),
             pltpu.VMEM((2, ROWS, Q_COLS), jnp.bfloat16),
             pltpu.SemaphoreType.DMA((2, chunks)),
             pltpu.SemaphoreType.DMA((2,)),
             pltpu.SemaphoreType.DMA((2, 4)),
+            pltpu.SemaphoreType.DMA((2, 4)),
+            pltpu.SemaphoreType.DMA((8, chunks, 4)),
             pltpu.SemaphoreType.DMA((2,)),
             pltpu.SemaphoreType.DMA((2,)),
             pltpu.SemaphoreType.DMA((2, ZS, 2)),
@@ -302,7 +324,7 @@
     scale = HEAD_DIM ** -0.5 * LOG2_E
 
     for slot in range(2 * SP):
-        where_piece[pos_all[slot // 2, 4 * (slot % 2), 0] // PIECE] = slot
+        where_piece[pos_all[slot // 2, slot % 2, 0] // PIECE] = slot
 
     def w_src(layer, ref, tile):
         return ref.at[layer, :, pl.ds(pl.multiple_of(tile * TILE, TILE), TILE)]

time: 282 us -> 271 us (0.961)
  Pallas kernels: 279 us -> 271 us
    pallas_call x1, Pallas kernels: 130 us -> 122 us  [gather_kv(): pl.pallas_call(gather_kernel, out_shape=(jax.ShapeDtypeStruct((2 * SP, PI...]
where the time goes in v4:
time: 271 us
  Pallas kernels  271 us (100%)
    pallas_call x1, Pallas kernels, decoder_layers(): pl.pallas_call(layers_kernel, out_shape=jax.ShapeDtypeStruct((ROWS, width...  149 us
    pallas_call x1, Pallas kernels, gather_kv(): pl.pallas_call(gather_kernel, out_shape=(jax.ShapeDtypeStruct((2 * SP, PI...  122 us

profile of v4, /device:TPU:0, one launch (start us, length us, event | category | flops | bytes accessed | tf_op | source)
XLA Modules:
  0.0 270.7 jit_solution(16762954701182403448)
XLA Ops:
  0.0 121.9 %gather_kv.1 = (bf16[16,128,3072]{2,1,0:T(8,128)(2,1)}, bf16[3072,2048]{1,0:T(8,128)(2,1)}, s32[8,2,128]{2,1,0:T(2,128)}, bf16[256,3072]{1,0:T(8,128)(2,1)}) custom-call(bf16[256,3072]{1,0:T(8,128)(2,1)} %x_ref.3, s32[2,128]{1,0:T(2,128)} %bitcast.4, bf16[3072]{0:T(1024)(128)(2,1)} %g_ref.1, bf16[3072,3072]{1,0:T(8,128)(2,1)} %wk_ref.1, ...), custom_call_target="tpu_custom_call" | custom-call | tf_op jit(solution)/shard_map/gather_kv/pallas_call | solution.py:276
  122.0 148.6 %layers.1 = bf16[256,3072]{1,0:T(8,128)(2,1)} custom-call(s32[8,2,128]{2,1,0:T(2,128)} %get-tuple-element.9.pos_all, s32[1,256]{1,0:T(1,128)} %bitcast.5, bf16[256,3072]{1,0:T(8,128)(2,1)} %x_ref.3, bf16[16,128,3072]{2,1,0:T(8,128)(2,1)} %get-tuple-element.10.k_ref, bf16[3072,2048]{1,0:T(8,128)(2,1)} %get-tuple-element.11.vt_ref, bf16[2,3072]{1,0:T(2,128)(2,1)} %ga_ref.3, ...), custom_call_target="tpu_custom_call" | custom-call | tf_op jit(solution)/shard_map/layers/pallas_call | solution.py:561

commit v5 on v4

--- a/solution.py
+++ b/solution.py
@@ -18,7 +18,7 @@
 HEADS_STEP = 4
 LANES_STEP = HEADS_STEP * HEAD_DIM
 TILE = 512
-W_SLOTS = 7
+W_SLOTS = 8
 D_SLOTS = 3
 KV_COLS = 768
 Q_COLS = 512
@@ -162,15 +162,19 @@
         far_src, far_half = remote_unit(z, jnp.maximum(unit - 2, 0))
         src = jnp.where(unit < 2, z, far_src)
         half = jnp.where(unit < 2, unit, far_half)
+
+        def normalise(lane):
+            def load(at):
+                return xbuf[lane, src, half, pl.ds(at, 16), :]
+
+            def store(at, value):
+                ubuf[pl.ds(pl.multiple_of(lane * PIECE + at, 16), 16), :] = value
+
+            norm_rows(load, store, gain, PIECE)
+
+        normalise(core)
         x_send(other, src, half, send_sib, sib).wait_recv()
-        for lane in range(2):
-            def load(at, lane=lane):
-                return xbuf[lane, src, half, pl.ds(at, 16), :]
-
-            def store(at, value, lane=lane):
-                ubuf[pl.ds(lane * PIECE + at, 16), :] = value
-
-            norm_rows(load, store, gain, PIECE)
+        normalise(other)
 
         def chunk_step(n, carry):
             par = (unit * chunks + n) % 2

time: 271 us -> 271 us (level)
  no operation moved by 1% of the time
where the time goes in v5:
time: 271 us; the launch traced here: 270 us
  Pallas kernels  270 us (100%)
    pallas_call x1, Pallas kernels, decoder_layers(): pl.pallas_call(layers_kernel, out_shape=jax.ShapeDtypeStruct((ROWS, width...  149 us
    pallas_call x1, Pallas kernels, gather_kv(): pl.pallas_call(gather_kernel, out_shape=(jax.ShapeDtypeStruct((2 * SP, PI...  122 us

profile of v5, /device:TPU:0, one launch (start us, length us, event | category | flops | bytes accessed | tf_op | source)
XLA Modules:
  0.0 270.4 jit_solution(13124587730207520412)
XLA Ops:
  0.0 121.5 %gather_kv.1 = (bf16[16,128,3072]{2,1,0:T(8,128)(2,1)}, bf16[3072,2048]{1,0:T(8,128)(2,1)}, s32[8,2,128]{2,1,0:T(2,128)}, bf16[256,3072]{1,0:T(8,128)(2,1)}) custom-call(bf16[256,3072]{1,0:T(8,128)(2,1)} %x_ref.3, s32[2,128]{1,0:T(2,128)} %bitcast.4, bf16[3072]{0:T(1024)(128)(2,1)} %g_ref.1, bf16[3072,3072]{1,0:T(8,128)(2,1)} %wk_ref.1, ...), custom_call_target="tpu_custom_call" | custom-call | tf_op jit(solution)/shard_map/gather_kv/pallas_call | solution.py:280
  121.5 148.7 %layers.1 = bf16[256,3072]{1,0:T(8,128)(2,1)} custom-call(s32[8,2,128]{2,1,0:T(2,128)} %get-tuple-element.9.pos_all, s32[1,256]{1,0:T(1,128)} %bitcast.5, bf16[256,3072]{1,0:T(8,128)(2,1)} %x_ref.3, bf16[16,128,3072]{2,1,0:T(8,128)(2,1)} %get-tuple-element.10.k_ref, bf16[3072,2048]{1,0:T(8,128)(2,1)} %get-tuple-element.11.vt_ref, bf16[2,3072]{1,0:T(2,128)(2,1)} %ga_ref.3, ...), custom_call_target="tpu_custom_call" | custom-call | tf_op jit(solution)/shard_map/layers/pallas_call | solution.py:565
